TPU v7x, 32 devices: a whole 2x2x4 slice. The times are simulated.
32 devices in a mesh: data: 2 (over x), node: 4 (over z), expert: 4 (over y, core).
Axes of the slice: x: 2, y: 2, z: 4, core: 2. Of those that a mesh axis runs over, the one named last changes fastest.
Arguments:
- tokens: bfloat16 [32768, 768], P(('data', 'node', 'expert')), parts along dimension 0
- expert_ids: int32 [32768, 1], P(('data', 'node', 'expert')), parts along dimension 0
- gate_weights: float32 [32768, 1], P(('data', 'node', 'expert')), parts along dimension 0
- slot_ids: int32 [32768, 1], P(('data', 'node', 'expert')), parts along dimension 0
- w_gate: bfloat16 [16, 768, 3072], P(('node', 'expert'))
- w_up: bfloat16 [16, 768, 3072], P(('node', 'expert'))
- w_down: bfloat16 [16, 3072, 768], P(('node', 'expert'))
Outputs:
- output: bfloat16 [32768, 768], P(('data', 'node', 'expert')), parts along dimension 0
There are 2 independent parts. A program takes and returns all parts, laid end to end along the dimension named above; an argument that names none is the same for every part.
All inputs are finite; a program needn't handle non-finite values.
Results may differ from a plain program's by a relative error of at most 0.001.
Values are sent between devices in bfloat16 or wider.
A program may use at most 1 GiB of HBM per device.

v0:
```python
import jax
import jax.numpy as jnp
from jax import lax
from jax.sharding import PartitionSpec as P

CAP_FACTOR = 2


def capacity(rows, top_k, experts):
    return ((CAP_FACTOR * rows * top_k + 8 * experts - 1) // (8 * experts)) * 8


def solution(mesh):
    group_axes = ("node", "expert")
    group_size = mesh.shape["node"] * mesh.shape["expert"]
    tok_spec = P(("data", "node", "expert"), None)
    weight_spec = P(("node", "expert"), None, None)

    def local_layer(tokens, expert_ids, gate_weights, slot_ids, w_gate, w_up, w_down):
        rows, width = tokens.shape
        top_k = expert_ids.shape[1]
        local_experts = w_gate.shape[0]
        experts = local_experts * group_size
        slot_count = capacity(rows, top_k, experts)
        flat_pos = jnp.where(slot_ids >= 0, expert_ids * slot_count + slot_ids, experts * slot_count)
        tok_index = jnp.broadcast_to(jnp.arange(rows, dtype=jnp.int32)[:, None], (rows, top_k))
        src_table = jnp.full((experts * slot_count,), rows, jnp.int32).at[flat_pos.reshape(-1)].set(tok_index.reshape(-1), mode="drop")
        send_buf = jnp.take(tokens, src_table, axis=0, mode="fill", fill_value=0)
        send_buf = send_buf.reshape(group_size, local_experts, 1, slot_count, width)
        recv_buf = lax.all_to_all(send_buf, group_axes, 0, 2, tiled=True)
        recv_buf = recv_buf.reshape(local_experts, group_size * slot_count, width)
        proj_gate = jnp.einsum("erd,edf->erf", recv_buf, w_gate, preferred_element_type=jnp.float32)
        proj_up = jnp.einsum("erd,edf->erf", recv_buf, w_up, preferred_element_type=jnp.float32)
        hidden = (jax.nn.silu(proj_gate) * proj_up).astype(jnp.bfloat16)
        expert_out = jnp.einsum("erf,efd->erd", hidden, w_down, preferred_element_type=jnp.float32).astype(jnp.bfloat16)
        expert_out = expert_out.reshape(local_experts, group_size, slot_count, width)
        returned = lax.all_to_all(expert_out, group_axes, 1, 0, tiled=True)
        returned = returned.reshape(experts * slot_count, width)
        picked = jnp.take(returned, flat_pos, axis=0, mode="fill", fill_value=0)
        combined = jnp.sum(gate_weights[:, :, None] * picked.astype(jnp.float32), axis=1)
        return combined.astype(jnp.bfloat16)

    return jax.shard_map(local_layer, mesh=mesh, in_specs=(tok_spec, tok_spec, tok_spec, tok_spec, weight_spec, weight_spec, weight_spec), out_specs=tok_spec, check_vma=False)
```

profile of v0, /device:TPU:11, one launch (start us, length us, event | category | flops | bytes accessed | tf_op | source)
XLA Modules:
  0.0 217.6 jit_solution(9895047008580233123)
XLA Ops:
  0.0 0.0 copy-start
  0.0 0.9 and_reduce_fusion
  0.9 4.3 %scatter_custom_fusion = s32[2048]{0:T(1024)S(1)} fusion(s32[1024]{0:T(1024)S(1)} %bitcast.33, s32[1024]{0:T(1024)S(1)} %iota.3, s32[]{:T(128)} %constant.24.clone.1), kind=kCustom, calls=%fused_computation.18 | custom fusion | bytes 8196 | tf_op jit(solution)/shard_map/scatter | solution.py:27
  5.2 0.0 copy-done
  5.2 9.4 %gather_fusion = bf16[2048,768]{1,0:T(8,128)(2,1)} fusion(bf16[1024,768]{1,0:T(8,128)(2,1)S(1)} %copy-done, s32[2048]{0:T(1024)S(1)} %fusion.11), kind=kCustom, calls=%fused_computation | custom fusion | bytes 6299648 | tf_op jit(solution)/shard_map/jit(_take)/gather | solution.py:28
  14.7 2.1 broadcast_select_fusion
  16.8 0.0 copy-start.3
  16.8 76.2 %all_to_all.8 = bf16[16,1,1,128,768]{4,3,2,1,0:T(8,128)(2,1)S(1)} all-to-all(bf16[16,1,1,128,768]{4,3,2,1,0:T(8,128)(2,1)S(1)} %broadcast_select_fusion), channel_id=1, replica_groups=mesh['data'=2,'node'=4,'expert'=4] {'node','expert'}, dimensions={0} | all-to-all | bytes 6291456 | tf_op jit(solution)/shard_map/all_to_all | solution.py:30
  93.0 0.0 copy-start.1
  93.0 1.7 copy-done.1
  94.7 0.0 copy-done.3
  94.7 13.3 %fusion.4 = f32[2048,3072]{1,0:T(8,128)} fusion(bf16[2048,768]{1,0:T(8,128)(2,1)S(1)} %bitcast.31, bf16[1,768,3072]{2,1,0:T(8,128)(2,1)S(1)} %copy-done.3), kind=kOutput, calls=%fused_computation.7 | convolution fusion | flops 9663676416 | bytes 33030144 | tf_op jit(solution)/shard_map/erd,edf->erf/dot_general | solution.py:32
  108.0 28.4 %fusion.6 = bf16[2048,768]{1,0:T(8,128)(2,1)} fusion(bf16[1,3072,768]{2,1,0:T(8,128)(2,1)} %param.13, f32[2048,3072]{1,0:T(8,128)} %fusion.4, bf16[2048,768]{1,0:T(8,128)(2,1)} %bitcast.32, bf16[1,768,3072]{2,1,0:T(8,128)(2,1)} %param.12), kind=kOutput, calls=%fused_computation.9 | convolution fusion | flops 19366674432 | bytes 40894464 | tf_op jit(solution)/shard_map/erf,efd->erd/dot_general | solution.py:35
  136.3 5.4 %all-to-all-start.1 = ((bf16[1,16,128,768]{3,2,0,1:T(8,128)(2,1)}), bf16[1,16,128,768]{3,2,0,1:T(8,128)(2,1)}, u32[]{:S(2)}, u32[]{:S(2)}) async-start(bf16[1,16,128,768]{3,2,0,1:T(8,128)(2,1)} %bitcast.30), calls=%async_computation.1 | async-start | bytes 6291456 | tf_op jit(solution)/shard_map/all_to_all | solution.py:37
  141.8 67.5 %all-to-all-done.1 = bf16[1,16,128,768]{3,2,0,1:T(8,128)(2,1)} async-done(((bf16[1,16,128,768]{3,2,0,1:T(8,128)(2,1)}), bf16[1,16,128,768]{3,2,0,1:T(8,128)(2,1)}, u32[]{:S(2)}, u32[]{:S(2)}) %all-to-all-start.1) | async-done | bytes 3145760 | tf_op jit(solution)/shard_map/all_to_all | solution.py:37
  209.2 0.0 copy-start.2
  209.2 6.8 %gather_fusion.1 = bf16[1024,768]{1,0:T(8,128)(2,1)S(1)} fusion(bf16[2048,768]{1,0:T(8,128)(2,1)} %bitcast.11, s32[1024]{0:T(1024)S(1)} %broadcast_clamp_fusion), kind=kCustom, calls=%fused_computation.1 | custom fusion | bytes 3149824 | tf_op jit(solution)/shard_map/jit(_take)/gather | solution.py:39
  216.0 0.0 copy-done.2
  216.0 1.6 multiply_convert_fusion.1
  (4 shorter events, 0.0 us)
Async XLA Ops:
  0.0 5.2 %copy-start = (bf16[1024,768]{1,0:T(8,128)(2,1)S(1)}, bf16[1024,768]{1,0:T(8,128)(2,1)}, u32[]{:S(2)}) copy-start(bf16[1024,768]{1,0:T(8,128)(2,1)} %param.7) | copy-start | bytes 4718596
  16.8 77.9 %copy-start.3 = (bf16[1,768,3072]{2,1,0:T(8,128)(2,1)S(1)}, bf16[1,768,3072]{2,1,0:T(8,128)(2,1)}, u32[]{:S(2)}) copy-start(bf16[1,768,3072]{2,1,0:T(8,128)(2,1)} %param.11) | copy-start | bytes 14155780
  93.0 1.7 copy-start.1
  136.3 72.9 %all-to-all-start.1 = ((bf16[1,16,128,768]{3,2,0,1:T(8,128)(2,1)}), bf16[1,16,128,768]{3,2,0,1:T(8,128)(2,1)}, u32[]{:S(2)}, u32[]{:S(2)}) async-start(bf16[1,16,128,768]{3,2,0,1:T(8,128)(2,1)} %bitcast.30), calls=%async_computation.1 | async-start | bytes 6291456 | tf_op jit(solution)/shard_map/all_to_all | solution.py:37
  209.2 6.8 %copy-start.2 = (f32[1024,1]{0,1:T(1,128)S(1)}, f32[1024,1]{0,1:T(1,128)}, u32[]{:S(2)}) copy-start(f32[1024,1]{0,1:T(1,128)} %param.9) | copy-start | bytes 12292
where the time goes:
time: 221 us; the launch traced here: 218 us
  blocking collectives  76.2 us (34%)
  waiting for transfers between devices  67.5 us (31%)
  matrix products  41.6 us (19%)
  local copies, waits for them, and re-layouts  22.3 us (10%)
  starting transfers between devices  5.43 us (2%)
  other arithmetic  4.57 us (2%)
    all_to_all x1, blocking collectives, local_layer(): recv_buf = lax.all_to_all(send_buf, group_axes, 0, 2, tiled=True)  76.2 us
    all_to_all x1, waiting for transfers between devices, local_layer(): returned = lax.all_to_all(expert_out, group_axes, 1, 0, tiled=True)  67.5 us
    dot_general x1, matrix products, local_layer(): jnp.einsum('erf,efd->erd', hidden, w_down, preferred_element_type=jnp.flo...  28.4 us
    dot_general x1, matrix products, local_layer(): jnp.einsum('erd,edf->erf', recv_buf, w_gate, preferred_element_type=jnp.f...  13.3 us
    gather x1, local copies, waits for them, and re-layouts, local_layer(): send_buf = jnp.take(tokens, src_table, axis=0, mode='fill', fill_value=0)  9.42 us
    gather x1, local copies, waits for them, and re-layouts, local_layer(): picked = jnp.take(returned, flat_pos, axis=0, mode='fill', fill_value=0)  6.78 us
    all_to_all x1, starting transfers between devices, local_layer(): returned = lax.all_to_all(expert_out, group_axes, 1, 0, tiled=True)  5.43 us
  transfers between devices with their start and end apart: 1, of which 1 were waited for; matrix products, arithmetic and copies ran while one was open for 0% of the time, Pallas kernels for 0%

commit v1 on v0

v1 whole, which is shorter than its diff:
```python
import functools

import jax
import jax.numpy as jnp
from jax import lax
from jax.experimental import pallas as pl
from jax.experimental.pallas import tpu as pltpu
from jax.sharding import PartitionSpec as P

CAP_FACTOR = 2
MESH = pl.DeviceIdType.MESH
FF_TILE = 512
REMOTE = 12


def capacity(rows, top_k, experts):
    return ((CAP_FACTOR * rows * top_k + 8 * experts - 1) // (8 * experts)) * 8


def flip(value, by):
    return 2 * ((value // 2 + by // 2) % 2) + (value + by) % 2


def partner(step):
    node, expert = lax.axis_index("node"), lax.axis_index("expert")
    far = 1 - step // REMOTE
    by_node = far * (1 + (step % 3 + 1) % 3)
    by_expert = far * (step // 3) + (1 - far) * (step - REMOTE)
    return flip(node, by_node), flip(expert, by_expert)


def layer_kernel(slot_count, tok_ref, pos_row_ref, pos_col_ref, gate_hbm, up_hbm, down_hbm, out_ref,
                 gate_w, up_w, down_w, send, recv, result, back, hidden, total,
                 w_sem, go_sem, come_sem, ret_go_sem, ret_come_sem):
    rows, width = tok_ref.shape
    steps = 16
    loads = [pltpu.make_async_copy(src.at[0], dst, w_sem.at[i]) for i, (src, dst) in enumerate(
        ((gate_hbm, gate_w), (up_hbm, up_w), (down_hbm, down_w)))]
    for load in loads:
        load.start()

    barrier = pltpu.get_barrier_semaphore()

    def greet(step, carry):
        node, expert = partner(step)
        pl.semaphore_signal(barrier, inc=1, device_id={"node": node, "expert": expert}, device_id_type=MESH)
        return carry

    lax.fori_loop(0, REMOTE, greet, 0)
    lax.fori_loop(REMOTE + 1, steps, greet, 0)

    def dispatch_copy(step):
        node, expert = partner(step)
        return pltpu.make_async_remote_copy(
            src_ref=send.at[step], dst_ref=recv.at[step], send_sem=go_sem.at[step], recv_sem=come_sem.at[step],
            device_id={"node": node, "expert": expert}, device_id_type=MESH)

    def return_copy(step):
        node, expert = partner(step)
        return pltpu.make_async_remote_copy(
            src_ref=result.at[step], dst_ref=back.at[step], send_sem=ret_go_sem.at[step], recv_sem=ret_come_sem.at[step],
            device_id={"node": node, "expert": expert}, device_id_type=MESH)

    def pick(step):
        node, expert = partner(step)
        first = (node * 4 + expert) * slot_count
        slot = lax.broadcasted_iota(jnp.int32, (slot_count, rows), 0) + first
        chosen = (pos_row_ref[...] == slot).astype(jnp.float32).astype(jnp.bfloat16)
        return jnp.dot(chosen, tok_ref[...], preferred_element_type=jnp.float32).astype(jnp.bfloat16)

    send[0] = pick(0)
    pl.semaphore_wait(barrier, steps - 1)
    dispatch_copy(0).start()

    def dispatch(step, carry):
        send[step] = pick(step)
        dispatch_copy(step).start()
        return carry

    lax.fori_loop(1, REMOTE, dispatch, 0)
    lax.fori_loop(REMOTE + 1, steps, dispatch, 0)
    recv[REMOTE] = pick(REMOTE)
    for load in loads:
        load.wait()

    def ffn(step, dst):
        block = recv[step]
        ff = hidden.shape[1]
        for start in range(0, ff, FF_TILE):
            cols = slice(start, start + FF_TILE)
            gate = jnp.dot(block, gate_w[:, cols], preferred_element_type=jnp.float32)
            up = jnp.dot(block, up_w[:, cols], preferred_element_type=jnp.float32)
            hidden[:, cols] = (jax.nn.silu(gate) * up).astype(jnp.bfloat16)
        dst[step] = jnp.dot(hidden[...], down_w[...], preferred_element_type=jnp.float32).astype(jnp.bfloat16)

    def compute(order, carry):
        step = (order + REMOTE) % steps

        @pl.when(step != REMOTE)
        def _():
            dispatch_copy(step).wait_recv()

        ffn(step, result)

        @pl.when(step != REMOTE)
        def _():
            return_copy(step).start()

        return carry

    lax.fori_loop(0, steps, compute, 0)
    back[REMOTE] = result[REMOTE]

    group = 4
    total[...] = jnp.zeros_like(total)

    def combine(order, carry):
        base = ((order + REMOTE // group) % (steps // group)) * group
        picks = []
        for i in range(group):
            step = base + i

            @pl.when(step != REMOTE)
            def _():
                return_copy(step).wait_recv()

            node, expert = partner(step)
            first = (node * 4 + expert) * slot_count
            slot = lax.broadcasted_iota(jnp.int32, (rows, slot_count), 1) + first
            picks.append((pos_col_ref[...] == slot).astype(jnp.float32).astype(jnp.bfloat16))
        chosen = jnp.concatenate(picks, axis=1)
        rets = back[pl.ds(base, group)].reshape(group * slot_count, width)
        total[...] += jnp.dot(chosen, rets, preferred_element_type=jnp.float32)
        return carry

    lax.fori_loop(0, steps // group, combine, 0)
    out_ref[...] = total[...].astype(out_ref.dtype)

    def drain(step, carry):
        dispatch_copy(step).wait_send()
        return_copy(step).wait_send()
        return carry

    lax.fori_loop(0, REMOTE, drain, 0)
    lax.fori_loop(REMOTE + 1, steps, drain, 0)


def solution(mesh):
    group_size = mesh.shape["node"] * mesh.shape["expert"]
    tok_spec = P(("data", "node", "expert"), None)
    weight_spec = P(("node", "expert"), None, None)

    def local_layer(tokens, expert_ids, gate_weights, slot_ids, w_gate, w_up, w_down):
        rows, width = tokens.shape
        ff = w_gate.shape[2]
        slot_count = capacity(rows, 1, group_size)
        flat_pos = jnp.where(slot_ids >= 0, expert_ids * slot_count + slot_ids, group_size * slot_count)
        vmem = pl.BlockSpec(memory_space=pltpu.VMEM)
        hbm = pl.BlockSpec(memory_space=pl.ANY)
        block = (group_size, slot_count, width)
        picked = pl.pallas_call(
            functools.partial(layer_kernel, slot_count),
            out_shape=jax.ShapeDtypeStruct((rows, width), jnp.bfloat16),
            in_specs=[vmem] * 3 + [hbm] * 3,
            out_specs=vmem,
            scratch_shapes=[
                pltpu.VMEM((width, ff), jnp.bfloat16),
                pltpu.VMEM((width, ff), jnp.bfloat16),
                pltpu.VMEM((ff, width), jnp.bfloat16),
                pltpu.VMEM(block, jnp.bfloat16),
                pltpu.VMEM(block, jnp.bfloat16),
                pltpu.VMEM(block, jnp.bfloat16),
                pltpu.VMEM(block, jnp.bfloat16),
                pltpu.VMEM((slot_count, ff), jnp.bfloat16),
                pltpu.VMEM((rows, width), jnp.float32),
                pltpu.SemaphoreType.DMA((3,)),
                pltpu.SemaphoreType.DMA((group_size,)),
                pltpu.SemaphoreType.DMA((group_size,)),
                pltpu.SemaphoreType.DMA((group_size,)),
                pltpu.SemaphoreType.DMA((group_size,)),
            ],
            compiler_params=pltpu.CompilerParams(
                collective_id=0, has_side_effects=True, vmem_limit_bytes=60 * 1024 * 1024),
            name="moe_layer",
        )(tokens, flat_pos.reshape(1, rows), flat_pos, w_gate, w_up, w_down)
        return (gate_weights * picked.astype(jnp.float32)).astype(jnp.bfloat16)

    return jax.shard_map(local_layer, mesh=mesh, in_specs=(tok_spec,) * 4 + (weight_spec,) * 3,
                         out_specs=tok_spec, check_vma=False)
```

time: 221 us -> 154 us (0.70); the launches traced: 218 us -> 154 us
  Pallas kernels: 0 us -> 147 us
  blocking collectives: 76.2 us -> 0 us
  waiting for transfers between devices: 67.5 us -> 0 us
  matrix products: 41.6 us -> 0 us
  local copies, waits for them, and re-layouts: 22.3 us -> 1.42 us
  starting transfers between devices: 5.43 us -> 0 us
    pallas_call x0 -> x1, Pallas kernels: none -> 147 us  [local_layer(): pl.pallas_call(functools.partial(layer_kernel, slot_count), out_shape=jax...]
    all_to_all x1 -> x0, blocking collectives: 76.2 us -> none  [local_layer(): recv_buf = lax.all_to_all(send_buf, group_axes, 0, 2, tiled=True)]
    all_to_all x1 -> x0, waiting for transfers between devices: 67.5 us -> none  [local_layer(): returned = lax.all_to_all(expert_out, group_axes, 1, 0, tiled=True)]
    dot_general x2 -> x0, matrix products: 41.6 us -> none  [the longest x1 28.4 us: local_layer(): jnp.einsum('erf,efd->erd', hidden, w_down, preferred_element_type=jnp.flo...]
    gather x2 -> x0, local copies, waits for them, and re-layouts: 16.2 us -> none  [the longest x1 9.42 us: local_layer(): send_buf = jnp.take(tokens, src_table, axis=0, mode='fill', fill_value=0)]
    all_to_all x1 -> x0, starting transfers between devices: 5.43 us -> none  [local_layer(): returned = lax.all_to_all(expert_out, group_axes, 1, 0, tiled=True)]
    scatter x1 -> x0, local copies, waits for them, and re-layouts: 4.32 us -> none  [local_layer(): jnp.full((experts * slot_count,), rows, jnp.int32).at[flat_pos.reshape(-1)]]
  transfers between devices with their start and end apart: 1 -> 0, of which waited for: 1 -> 0; matrix products, arithmetic and copies ran while one was open for 0% -> 0% of each run, Pallas kernels for 0% -> 0%
where the time goes in v1:
time: 154 us
  Pallas kernels  147 us (95%)
  other arithmetic  5.73 us (4%)
    pallas_call x1, Pallas kernels, local_layer(): pl.pallas_call(functools.partial(layer_kernel, slot_count), out_shape=jax...  147 us

profile of v1, /device:TPU:11, one launch (start us, length us, event | category | flops | bytes accessed | tf_op | source)
XLA Modules:
  0.0 154.0 jit_solution(10503928867856694658)
XLA Ops:
  0.0 0.7 broadcast_multiply_fusion
  0.7 0.7 broadcast_compare_fusion
  1.4 0.3 copy.20
  1.7 0.2 copy.18
  1.9 0.9 copy.19
  2.8 1.5 fusion
  4.3 0.0 copy-start
  4.3 146.8 %moe_layer.1 = bf16[1024,768]{1,0:T(8,128)(2,1)} custom-call(bf16[1024,768]{1,0:T(8,128)(2,1)} %tok_ref.1, s32[1,1024]{1,0:T(1,128)} %bitcast.2, s32[1024,1]{1,0:T(8,128)} %get-tuple-element.6.pos_col_ref, bf16[1,768,3072]{2,1,0:T(8,128)(2,1)} %gate_hbm.1, bf16[1,768,3072]{2,1,0:T(8,128)(2,1)} %up_hbm.1, bf16[1,3072,768]{2,1,0:T(8,128)(2,1)} %down_hbm.1), custom_call_target="tpu_custom_call" | custom-call | tf_op jit(solution)/shard_map/moe_layer/pallas_call | solution.py:161
  151.2 0.0 copy-done
  151.2 2.9 %multiply_convert_fusion = bf16[1024,768]{1,0:T(8,128)(2,1)} fusion(bf16[1024,768]{1,0:T(8,128)(2,1)} %moe_layer.1, f32[1024]{0:T(1024)S(1)} %bitcast.3), kind=kLoop, calls=%fused_computation | loop fusion | flops 2359296 | bytes 3149824 | tf_op jit(solution)/shard_map/convert_element_type | solution.py:186
Async XLA Ops:
  4.3 146.9 %copy-start = (f32[1024,1]{0,1:T(1,128)S(1)}, f32[1024,1]{0,1:T(1,128)}, u32[]{:S(2)}) copy-start(f32[1024,1]{0,1:T(1,128)} %param.9) | copy-start | bytes 12292

commit v2 on v0

v2 whole, which is shorter than its diff:
```python
import functools

import jax
import jax.numpy as jnp
from jax import lax
from jax.experimental import pallas as pl
from jax.experimental.pallas import tpu as pltpu
from jax.sharding import PartitionSpec as P

CAP_FACTOR = 2
MESH = pl.DeviceIdType.MESH
FF_TILE = 512
REMOTE = 12
BASE = 64
SPILL = 224
LIST = SPILL + 16
PADDED = 256


def capacity(rows, top_k, experts):
    return ((CAP_FACTOR * rows * top_k + 8 * experts - 1) // (8 * experts)) * 8


def flip(value, by):
    return 2 * ((value // 2 + by // 2) % 2) + (value + by) % 2


def place(by_node, by_expert):
    return {"node": flip(lax.axis_index("node"), by_node), "expert": flip(lax.axis_index("expert"), by_expert)}


def expert_of(by_node, by_expert):
    at = place(by_node, by_expert)
    return at["node"] * 4 + at["expert"]


def one_hot(mask):
    return mask.astype(jnp.float32).astype(jnp.bfloat16)


def matmul(a, b):
    return jnp.dot(a, b, preferred_element_type=jnp.float32)


def matmul_t(a, b):
    return lax.dot_general(a, b, (((0,), (0,)), ((), ())), preferred_element_type=jnp.float32)


def expert_ffn(block, gate_w, up_w, down_w, hidden):
    for start in range(0, hidden.shape[1], FF_TILE):
        cols = slice(start, start + FF_TILE)
        gate = matmul(block, gate_w[:, cols])
        up = matmul(block, up_w[:, cols])
        hidden[:, cols] = (jax.nn.silu(gate) * up).astype(jnp.bfloat16)
    return matmul(hidden[...], down_w[...]).astype(jnp.bfloat16)


def load_weights(refs, scratch, sems):
    loads = [pltpu.make_async_copy(src.at[0], dst, sems.at[i]) for i, (src, dst) in enumerate(zip(refs, scratch))]
    for load in loads:
        load.start()
    return loads


def remote(src, dst, go, come, device):
    return pltpu.make_async_remote_copy(
        src_ref=src, dst_ref=dst, send_sem=go, recv_sem=come, device_id=device, device_id_type=MESH)


def padded_kernel(slot_count, tok_ref, ids_ref, slots_ref, gate_hbm, up_hbm, down_hbm, out_ref,
                  gate_w, up_w, down_w, send, recv, result, back, hidden, total,
                  w_sem, go_sem, come_sem, ret_go_sem, ret_come_sem):
    rows, width = tok_ref.shape
    steps = 16
    loads = load_weights((gate_hbm, up_hbm, down_hbm), (gate_w, up_w, down_w), w_sem)
    barrier = pltpu.get_barrier_semaphore()

    def relative(step):
        far = 1 - step // REMOTE
        return far * (1 + (step % 3 + 1) % 3), far * (step // 3) + (1 - far) * (step - REMOTE)

    def greet(step, carry):
        pl.semaphore_signal(barrier, inc=1, device_id=place(*relative(step)), device_id_type=MESH)
        return carry

    lax.fori_loop(0, REMOTE, greet, 0)
    lax.fori_loop(REMOTE + 1, steps, greet, 0)

    def dispatch_copy(step):
        return remote(send.at[step], recv.at[step], go_sem.at[step], come_sem.at[step], place(*relative(step)))

    def return_copy(step):
        return remote(result.at[step], back.at[step], ret_go_sem.at[step], ret_come_sem.at[step], place(*relative(step)))

    flat_pos = jnp.where(slots_ref[...] >= 0, ids_ref[...] * slot_count + slots_ref[...], steps * slot_count)

    def choice(step):
        first = expert_of(*relative(step)) * slot_count
        return one_hot(flat_pos == lax.broadcasted_iota(jnp.int32, (slot_count, rows), 0) + first)

    def pick(step):
        return matmul(choice(step), tok_ref[...]).astype(jnp.bfloat16)

    pl.semaphore_wait(barrier, steps - 1)

    def dispatch(step, carry):
        send[step] = pick(step)
        dispatch_copy(step).start()
        return carry

    lax.fori_loop(0, REMOTE, dispatch, 0)
    lax.fori_loop(REMOTE + 1, steps, dispatch, 0)
    recv[REMOTE] = pick(REMOTE)
    for load in loads:
        load.wait()

    def compute(order, carry):
        step = (order + REMOTE) % steps

        @pl.when(step != REMOTE)
        def _():
            dispatch_copy(step).wait_recv()

        result[step] = expert_ffn(recv[step], gate_w, up_w, down_w, hidden)

        @pl.when(step != REMOTE)
        def _():
            return_copy(step).start()

        return carry

    lax.fori_loop(0, steps, compute, 0)
    back[REMOTE] = result[REMOTE]
    total[...] = jnp.zeros_like(total)

    def combine(order, carry):
        step = (order + REMOTE) % steps

        @pl.when(step != REMOTE)
        def _():
            return_copy(step).wait_recv()

        total[...] += matmul_t(choice(step), back[step])
        return carry

    lax.fori_loop(0, steps, combine, 0)
    out_ref[...] = total[...].astype(out_ref.dtype)

    def drain(step, carry):
        dispatch_copy(step).wait_send()
        return_copy(step).wait_send()
        return carry

    lax.fori_loop(0, REMOTE, drain, 0)
    lax.fori_loop(REMOTE + 1, steps, drain, 0)


def packed_kernel(slot_count, tok_ref, ids_ref, slots_ref, gate_hbm, up_hbm, down_hbm, out_ref, full_ref,
                  gate_w, up_w, down_w, hidden, total,
                  own_hot, own_send, own_recv, own_result, own_back,
                  z_hot, z_send, z_recv, z_result, z_back,
                  list_hot, list_send, lists, shares, core_in, y_in, z_in, list_back,
                  flag_src, flags, group_src, group_in,
                  w_sem, own_sem, z_sem, list_sem, share_sem, flag_sem):
    rows, width = tok_ref.shape
    node, expert = lax.axis_index("node"), lax.axis_index("expert")
    inner = (node + 1) // 2 == 1
    loads = load_weights((gate_hbm, up_hbm, down_hbm), (gate_w, up_w, down_w), w_sem)

    barrier = pltpu.get_barrier_semaphore()
    twin = {"data": (lax.axis_index("data") + 1) % 2}
    pl.semaphore_signal(barrier, inc=1, device_id=twin, device_id_type=MESH)

    def greet(q, carry):
        pl.semaphore_signal(barrier, inc=1, device_id=place(q // 4, q % 4), device_id_type=MESH)
        return carry

    lax.fori_loop(1, 16, greet, 0)

    def own_copy(w):
        return remote(own_send.at[w], own_recv.at[w], own_sem.at[0, w], own_sem.at[1, w], place(0, w))

    def own_return(w):
        return remote(own_result.at[w], own_back.at[w], own_sem.at[2, w], own_sem.at[3, w], place(0, w))

    def z_part(k):
        return pl.ds(k * BASE, BASE) if k < 2 else pl.ds(2 * BASE, slot_count)

    def z_copy(w, k):
        return remote(z_send.at[w, z_part(k)], z_recv.at[w, z_part(k)], z_sem.at[0, 3 * w + k], z_sem.at[1, 3 * w + k],
                      place((2, 3, 1)[k], w))

    def z_return(w, k):
        return remote(z_result.at[w, z_part(k)], z_back.at[w, z_part(k)], z_sem.at[2, 3 * w + k], z_sem.at[3, 3 * w + k],
                      place((2, 3, 1)[k], w))

    sent = pl.ds(0, LIST)
    gate_node = {"node": 2 - node // 2, "expert": expert}
    kind = 1 - ((node + 1) // 2 + 1) % 2

    def list_out():
        return remote(list_send.at[sent], lists.at[0, kind, sent], list_sem.at[8], list_sem.at[kind], gate_node)

    def forward_z(i):
        return remote(lists.at[0, i, sent], lists.at[0, 1 - i, sent], list_sem.at[9 + i], list_sem.at[1 - i], place(1, 0))

    def forward_y(i):
        return remote(lists.at[0, i, sent], lists.at[2, i, sent], list_sem.at[11 + i], list_sem.at[4 + i], place(0, 2))

    def forward_core(w, i):
        return remote(lists.at[w, i, sent], lists.at[w + 1, i, sent], list_sem.at[13 + w + i], list_sem.at[2 * w + 2 + i],
                      place(0, 1))

    def arrived(w, i):
        return remote(lists.at[w, i, sent], lists.at[w, i, sent], list_sem.at[8], list_sem.at[2 * w + i], place(0, 1))

    def share_core(w, i):
        return remote(shares.at[w, i, sent], core_in.at[w // 2, i, sent], share_sem.at[2 * w + i],
                      share_sem.at[8 + 2 * (w // 2) + i], place(0, 1))

    def share_y(i):
        return remote(shares.at[2, i, sent], y_in.at[i, sent], share_sem.at[4 + i], share_sem.at[12 + i], place(0, 2))

    def share_z(i):
        return remote(shares.at[0, i, sent], z_in.at[1 - i, sent], share_sem.at[i], share_sem.at[15 - i], place(1, 0))

    def share_home(i):
        return remote(shares.at[0, i, sent], list_back.at[sent], share_sem.at[i], share_sem.at[16], place(2 + i, 0))

    def flag_copy(q):
        return remote(flag_src, flags.at[q], flag_sem.at[0, q], flag_sem.at[1, q], place(q // 4, q % 4))

    def group_copy():
        return remote(group_src, group_in, flag_sem.at[0, 0], flag_sem.at[1, 0], twin)

    ids, slots = ids_ref[...], slots_ref[...]
    flat_pos = jnp.where(slots >= 0, ids * slot_count + slots, 16 * slot_count)
    spills = jnp.logical_and(ids // 8 != node // 2, slots >= BASE).astype(jnp.float32)
    lanes = 128
    folds = rows // lanes
    grid = jnp.concatenate([spills[:, i * lanes:(i + 1) * lanes] for i in range(folds)], axis=0)
    upto = one_hot(lax.broadcasted_iota(jnp.int32, (lanes, lanes), 0) <= lax.broadcasted_iota(jnp.int32, (lanes, lanes), 1))
    before = one_hot(lax.broadcasted_iota(jnp.int32, (folds, folds), 1) < lax.broadcasted_iota(jnp.int32, (folds, folds), 0))
    marks = grid.astype(jnp.bfloat16)
    order = matmul(marks, upto) + jnp.sum(matmul(before, marks), axis=1, keepdims=True)
    order = jnp.where(grid > 0, order, 0.0).astype(jnp.int32) - 1
    order = jnp.concatenate([order[i:i + 1, :] for i in range(folds)], axis=1)
    order = jnp.where(order < SPILL, order, -1)
    list_hot[...] = one_hot(order == lax.broadcasted_iota(jnp.int32, (PADDED, rows), 0))
    codes = jnp.concatenate([ids, slots] + [jnp.zeros_like(ids)] * 14, axis=0).astype(jnp.float32).astype(jnp.bfloat16)
    codes = lax.dot_general(codes, list_hot[...], (((1,), (1,)), ((), ())), preferred_element_type=jnp.float32)
    list_send[...] = matmul(list_hot[...], tok_ref[...]).astype(jnp.bfloat16)
    list_send[SPILL:LIST, 0:PADDED] = codes.astype(jnp.bfloat16)
    flag_src[...] = jnp.broadcast_to(jnp.maximum(jnp.sum(spills) - SPILL, 0.0), flag_src.shape)
    for w in range(4):
        for i in range(2):
            lists[w, i, LIST:PADDED] = jnp.zeros((PADDED - LIST, width), jnp.bfloat16)
    list_back[LIST:PADDED] = jnp.zeros((PADDED - LIST, width), jnp.bfloat16)

    pl.semaphore_wait(barrier, 16)
    list_out().start()

    def flag_out(q, carry):
        flag_copy(q).start()
        return carry

    lax.fori_loop(1, 16, flag_out, 0)

    def target(by_node, w, count):
        return lax.broadcasted_iota(jnp.int32, (count, rows), 0) + expert_of(by_node, w) * slot_count

    def own_pick(w, carry):
        own_hot[w] = one_hot(flat_pos == target(0, w, slot_count))
        own_send[w] = matmul(own_hot[w], tok_ref[...]).astype(jnp.bfloat16)

        @pl.when(w > 0)
        def _():
            own_copy(w).start()

        return carry

    def z_pick(w, carry):
        z_hot[w, 0:BASE] = one_hot(flat_pos == target(2, w, BASE))
        z_hot[w, BASE:2 * BASE] = one_hot(flat_pos == target(3, w, BASE))
        z_hot[w, 2 * BASE:] = one_hot(flat_pos == target(1, w, slot_count))
        z_send[w] = matmul(z_hot[w], tok_ref[...]).astype(jnp.bfloat16)
        for k in range(3):
            z_copy(w, k).start()
        return carry

    lax.fori_loop(0, 1, z_pick, 0)
    lax.fori_loop(0, 4, own_pick, 0)
    lax.fori_loop(1, 4, z_pick, 0)
    for load in loads:
        load.wait()

    def ffn(block):
        return expert_ffn(block, gate_w, up_w, down_w, hidden)

    def own_step(w, carry):
        @pl.when(w > 0)
        def _():
            own_copy(w).wait_recv()
            own_result[w] = ffn(own_recv[w])
            own_return(w).start()

        @pl.when(w == 0)
        def _():
            own_back[w] = ffn(own_send[w])

        return carry

    lax.fori_loop(0, 4, own_step, 0)

    def flag_in(q, carry):
        flag_copy(q).wait_recv()
        return carry

    lax.fori_loop(1, 16, flag_in, 0)
    flags[0] = flag_src[...]
    group_src[...] = jnp.max(flags[...], axis=0)

    me = node * 4 + expert

    def round_step(r, carry):
        @pl.when(r == 0)
        def _():
            for i in range(2):
                arrived(0, i).wait_recv()

                @pl.when(inner)
                def _():
                    forward_z(i).start()

                forward_core(0, i).start()
                forward_y(i).start()
            flag_copy(1).wait_send()
            group_copy().start()

        @pl.when(r == 1)
        def _():
            for i in range(2):
                arrived(2, i).wait_recv()
                forward_core(2, i).start()

        z_copy(r, 2).wait_recv()
        near = slice(2 * BASE, 2 * BASE + slot_count)
        far = slice(0, 2 * BASE)
        z_result[r, near] = ffn(z_recv[r, near])
        z_return(r, 2).start()
        z_copy(r, 0).wait_recv()
        z_copy(r, 1).wait_recv()
        z_result[r, far] = ffn(z_recv[r, far])
        z_return(r, 0).start()
        z_return(r, 1).start()

        w = (1 - r // 2) * (2 * r + 1) + (r // 2) * (6 - 2 * r)

        @pl.when(w % 2 == 1)
        def _():
            for i in range(2):
                arrived(w, i).wait_recv()

        mine, blocks = [], []
        for i in range(2):
            codes = lists[w, i, SPILL:LIST, 0:PADDED].astype(jnp.float32)
            slot = lax.broadcasted_iota(jnp.int32, (BASE, PADDED), 0) + BASE
            hit = jnp.logical_and(codes[0:1].astype(jnp.int32) == me, codes[1:2].astype(jnp.int32) == slot)
            mine.append(one_hot(hit))
            blocks.append(matmul(mine[i], lists[w, i]).astype(jnp.bfloat16))
        y = ffn(jnp.concatenate(blocks, axis=0))
        for i in range(2):
            shares[w, i] = matmul_t(mine[i], y[i * BASE:(i + 1) * BASE]).astype(jnp.bfloat16)

        @pl.when(w % 2 == 1)
        def _():
            for i in range(2):
                share_core(w, i).start()

        @pl.when(w == 2)
        def _():
            for i in range(2):
                share_core(3, i).wait_recv()
                shares[2, i, 0:LIST] += core_in[1, i, 0:LIST]
                share_y(i).start()

        return carry

    lax.fori_loop(0, 4, round_step, 0)

    for i in range(2):
        share_core(1, i).wait_recv()
        share_y(i).wait_recv()
        shares[0, i, 0:LIST] += core_in[0, i, 0:LIST] + y_in[i, 0:LIST]

    @pl.when(jnp.logical_not(inner))
    def _():
        for i in range(2):
            share_z(i).start()

    for w in range(1, 4):
        own_return(w).wait_recv()
    total[...] = matmul_t(own_hot[...].reshape(4 * slot_count, rows), own_back[...].reshape(4 * slot_count, width))

    @pl.when(inner)
    def _():
        for i in range(2):
            share_z(1 - i).wait_recv()
            shares[0, i, 0:LIST] += z_in[i, 0:LIST]
            share_home(i).start()

    def z_combine(w, carry):
        for k in (2, 0, 1):
            z_return(w, k).wait_recv()
        total[...] += matmul_t(z_hot[w], z_back[w])
        return carry

    lax.fori_loop(0, 4, z_combine, 0)
    share_home(0).wait_recv()
    total[...] += matmul_t(list_hot[...], list_back[...])
    out_ref[...] = total[...].astype(out_ref.dtype)

    group_copy().wait_recv()
    full_ref[0, 0] = (jnp.max(jnp.maximum(group_src[...], group_in[...])) > 0.0).astype(jnp.int32)

    for w in range(1, 4):
        own_copy(w).wait_send()
        own_return(w).wait_send()
    for w in range(4):
        for k in range(3):
            z_copy(w, k).wait_send()
            z_return(w, k).wait_send()
    list_out().wait_send()
    group_copy().wait_send()

    def flag_sent(q, carry):
        flag_copy(q).wait_send()
        return carry

    lax.fori_loop(2, 16, flag_sent, 0)
    for i in range(2):
        forward_y(i).wait_send()
        forward_core(0, i).wait_send()
        forward_core(2, i).wait_send()
        share_core(1, i).wait_send()
        share_core(3, i).wait_send()
        share_y(i).wait_send()

        @pl.when(inner)
        def _():
            forward_z(i).wait_send()
            share_home(i).wait_send()

        @pl.when(jnp.logical_not(inner))
        def _():
            share_z(i).wait_send()


def solution(mesh):
    group_size = mesh.shape["node"] * mesh.shape["expert"]
    tok_spec = P(("data", "node", "expert"), None)
    weight_spec = P(("node", "expert"), None, None)

    def local_layer(tokens, expert_ids, gate_weights, slot_ids, w_gate, w_up, w_down):
        rows, width = tokens.shape
        ff = w_gate.shape[2]
        slot_count = capacity(rows, 1, group_size)
        vmem = pl.BlockSpec(memory_space=pltpu.VMEM)
        smem = pl.BlockSpec(memory_space=pltpu.SMEM)
        hbm = pl.BlockSpec(memory_space=pl.ANY)
        dma = pltpu.SemaphoreType.DMA
        weights = [pltpu.VMEM((width, ff), jnp.bfloat16), pltpu.VMEM((width, ff), jnp.bfloat16),
                   pltpu.VMEM((ff, width), jnp.bfloat16)]
        hidden = pltpu.VMEM((slot_count, ff), jnp.bfloat16)
        total = pltpu.VMEM((rows, width), jnp.float32)
        picked_shape = jax.ShapeDtypeStruct((rows, width), jnp.bfloat16)
        operands = (tokens, expert_ids.reshape(1, rows), slot_ids.reshape(1, rows), w_gate, w_up, w_down)

        def bf16(*shape):
            return pltpu.VMEM(shape, jnp.bfloat16)

        def params(number):
            return pltpu.CompilerParams(collective_id=number, has_side_effects=True, vmem_limit_bytes=60 * 1024 * 1024)

        def scaled(picked):
            return (gate_weights * picked.astype(jnp.float32)).astype(jnp.bfloat16)

        def padded():
            block = (group_size, slot_count, width)
            return pl.pallas_call(
                functools.partial(padded_kernel, slot_count), out_shape=picked_shape,
                in_specs=[vmem] * 3 + [hbm] * 3, out_specs=vmem,
                scratch_shapes=weights + [bf16(*block)] * 4 + [hidden, total, dma((3,))] + [dma((group_size,))] * 4,
                compiler_params=params(1), name="padded_layer",
            )(*operands)

        own = (4, slot_count, width)
        zed = (4, 2 * BASE + slot_count, width)
        flag = pltpu.VMEM((8, 128), jnp.float32)
        picked, full = pl.pallas_call(
            functools.partial(packed_kernel, slot_count),
            out_shape=(picked_shape, jax.ShapeDtypeStruct((1, 1), jnp.int32)),
            in_specs=[vmem] * 3 + [hbm] * 3, out_specs=(vmem, smem),
            scratch_shapes=weights + [hidden, total]
            + [bf16(4, slot_count, rows)] + [bf16(*own)] * 4
            + [bf16(4, 2 * BASE + slot_count, rows)] + [bf16(*zed)] * 4
            + [bf16(PADDED, rows), bf16(PADDED, width), bf16(4, 2, PADDED, width), bf16(4, 2, PADDED, width),
               bf16(2, 2, PADDED, width), bf16(2, PADDED, width), bf16(2, PADDED, width), bf16(PADDED, width)]
            + [flag, pltpu.VMEM((16, 8, 128), jnp.float32), flag, flag]
            + [dma((3,)), dma((4, 4)), dma((4, 12)), dma((17,)), dma((17,)), dma((2, 16))],
            compiler_params=params(0), name="packed_layer",
        )(*operands)
        return lax.cond(full[0, 0] > 0, lambda: scaled(padded()), lambda: scaled(picked))

    return jax.shard_map(local_layer, mesh=mesh, in_specs=(tok_spec,) * 4 + (weight_spec,) * 3,
                         out_specs=tok_spec, check_vma=False)
```

time: 221 us -> 165 us (0.75)
  the two profiles are of different devices: /device:TPU:11 before, /device:TPU:16 now
where the time goes in v2:
time: 165 us
  Pallas kernels  163 us (99%)
    pallas_call x1, Pallas kernels, local_layer(): pl.pallas_call(functools.partial(packed_kernel, slot_count), out_shape=(p...  163 us

profile of v2, /device:TPU:16, one launch (start us, length us, event | category | flops | bytes accessed | tf_op | source)
XLA Modules:
  0.0 164.7 jit_solution(18355349231524460151)
XLA Ops:
  0.0 0.0 copy-start
  0.0 0.0 copy-start.1
  0.0 0.0 copy-start.2
  0.0 0.0 copy-start.3
  0.0 162.5 %packed_layer.1 = (bf16[1024,768]{1,0:T(8,128)(2,1)S(1)}, s32[1,1]{1,0:T(1,128)}) custom-call(bf16[1024,768]{1,0:T(8,128)(2,1)} %tok_ref.1, s32[1,1024]{1,0:T(1,128)} %bitcast.4, s32[1,1024]{1,0:T(1,128)} %bitcast.6, bf16[1,768,3072]{2,1,0:T(8,128)(2,1)} %gate_hbm.1, bf16[1,768,3072]{2,1,0:T(8,128)(2,1)} %up_hbm.1, bf16[1,3072,768]{2,1,0:T(8,128)(2,1)} %down_hbm.1), custom_call_target="tpu_custom_call" | custom-call | tf_op jit(solution)/shard_map/packed_layer/pallas_call | solution.py:500
  163.1 0.0 copy-done
  163.1 0.0 copy-done.1
  163.2 0.0 copy-done.2
  163.2 0.0 copy-done.3
  163.2 1.5 fusion
  (1 shorter events, 0.0 us)
Async XLA Ops:
  0.0 163.1 %copy-start = (bf16[1024,768]{1,0:T(8,128)(2,1)S(1)}, bf16[1024,768]{1,0:T(8,128)(2,1)}, u32[]{:S(2)}) copy-start(bf16[1024,768]{1,0:T(8,128)(2,1)} %tok_ref.1) | copy-start | bytes 4718596
  0.0 163.1 %copy-start.1 = (s32[1024,1]{0,1:T(1,128)S(1)}, s32[1024,1]{0,1:T(1,128)}, u32[]{:S(2)}) copy-start(s32[1024,1]{0,1:T(1,128)} %param.10) | copy-start | bytes 12292
  0.0 163.2 %copy-start.2 = (s32[1024,1]{0,1:T(1,128)S(1)}, s32[1024,1]{0,1:T(1,128)}, u32[]{:S(2)}) copy-start(s32[1024,1]{0,1:T(1,128)} %param.12) | copy-start | bytes 12292
  0.0 163.2 %copy-start.3 = (f32[1024,1]{0,1:T(1,128)S(1)}, f32[1024,1]{0,1:T(1,128)}, u32[]{:S(2)}) copy-start(f32[1024,1]{0,1:T(1,128)} %param.11) | copy-start | bytes 12292

commit v3 on v2

--- a/solution.py
+++ b/solution.py
@@ -12,7 +12,7 @@
 FF_TILE = 512
 REMOTE = 12
 BASE = 64
-SPILL = 224
+SPILL = 144
 LIST = SPILL + 16
 PADDED = 256
 
@@ -159,7 +159,7 @@
                   gate_w, up_w, down_w, hidden, total,
                   own_hot, own_send, own_recv, own_result, own_back,
                   z_hot, z_send, z_recv, z_result, z_back,
-                  list_hot, list_send, lists, shares, core_in, y_in, z_in, list_back,
+                  list_hot, list_send, lists, shares, core_in, z_in, list_back,
                   flag_src, flags, group_src, group_in,
                   w_sem, own_sem, z_sem, list_sem, share_sem, flag_sem):
     rows, width = tok_ref.shape
@@ -195,37 +195,34 @@
                       place((2, 3, 1)[k], w))
 
     sent = pl.ds(0, LIST)
-    gate_node = {"node": 2 - node // 2, "expert": expert}
     kind = 1 - ((node + 1) // 2 + 1) % 2
 
-    def list_out():
-        return remote(list_send.at[sent], lists.at[0, kind, sent], list_sem.at[8], list_sem.at[kind], gate_node)
-
-    def forward_z(i):
-        return remote(lists.at[0, i, sent], lists.at[0, 1 - i, sent], list_sem.at[9 + i], list_sem.at[1 - i], place(1, 0))
-
-    def forward_y(i):
-        return remote(lists.at[0, i, sent], lists.at[2, i, sent], list_sem.at[11 + i], list_sem.at[4 + i], place(0, 2))
-
-    def forward_core(w, i):
-        return remote(lists.at[w, i, sent], lists.at[w + 1, i, sent], list_sem.at[13 + w + i], list_sem.at[2 * w + 2 + i],
-                      place(0, 1))
+    def list_out(h):
+        return remote(list_send.at[h, sent], lists.at[2 * h, kind, sent], list_sem.at[8 + h], list_sem.at[4 * h + kind],
+                      {"node": 2 - node // 2, "expert": flip(expert, 2 * h)})
 
     def arrived(w, i):
         return remote(lists.at[w, i, sent], lists.at[w, i, sent], list_sem.at[8], list_sem.at[2 * w + i], place(0, 1))
+
+    def forward_z(w, i):
+        return remote(lists.at[w, i, sent], lists.at[w, 1 - i, sent], list_sem.at[10 + w + i],
+                      list_sem.at[2 * w + 1 - i], place(1, 0))
+
+    def forward_core(w, i):
+        return remote(lists.at[w, i, sent], lists.at[w + 1, i, sent], list_sem.at[14 + w + i],
+                      list_sem.at[2 * w + 2 + i], place(0, 1))
 
     def share_core(w, i):
         return remote(shares.at[w, i, sent], core_in.at[w // 2, i, sent], share_sem.at[2 * w + i],
                       share_sem.at[8 + 2 * (w // 2) + i], place(0, 1))
 
-    def share_y(i):
-        return remote(shares.at[2, i, sent], y_in.at[i, sent], share_sem.at[4 + i], share_sem.at[12 + i], place(0, 2))
-
-    def share_z(i):
-        return remote(shares.at[0, i, sent], z_in.at[1 - i, sent], share_sem.at[i], share_sem.at[15 - i], place(1, 0))
-
-    def share_home(i):
-        return remote(shares.at[0, i, sent], list_back.at[sent], share_sem.at[i], share_sem.at[16], place(2 + i, 0))
+    def share_z(w, i):
+        return remote(shares.at[w, i, sent], z_in.at[w // 2, 1 - i, sent], share_sem.at[2 * w + i],
+                      share_sem.at[13 + w - i], place(1, 0))
+
+    def share_home(w, i):
+        return remote(shares.at[w, i, sent], list_back.at[w // 2, sent], share_sem.at[2 * w + i],
+                      share_sem.at[16 + w // 2], place(2 + i, w))
 
     def flag_copy(q):
         return remote(flag_src, flags.at[q], flag_sem.at[0, q], flag_sem.at[1, q], place(q // 4, q % 4))
@@ -235,30 +232,36 @@
 
     ids, slots = ids_ref[...], slots_ref[...]
     flat_pos = jnp.where(slots >= 0, ids * slot_count + slots, 16 * slot_count)
-    spills = jnp.logical_and(ids // 8 != node // 2, slots >= BASE).astype(jnp.float32)
+    far_spill = jnp.logical_and(ids // 8 != node // 2, slots >= BASE)
     lanes = 128
     folds = rows // lanes
-    grid = jnp.concatenate([spills[:, i * lanes:(i + 1) * lanes] for i in range(folds)], axis=0)
     upto = one_hot(lax.broadcasted_iota(jnp.int32, (lanes, lanes), 0) <= lax.broadcasted_iota(jnp.int32, (lanes, lanes), 1))
     before = one_hot(lax.broadcasted_iota(jnp.int32, (folds, folds), 1) < lax.broadcasted_iota(jnp.int32, (folds, folds), 0))
-    marks = grid.astype(jnp.bfloat16)
-    order = matmul(marks, upto) + jnp.sum(matmul(before, marks), axis=1, keepdims=True)
-    order = jnp.where(grid > 0, order, 0.0).astype(jnp.int32) - 1
-    order = jnp.concatenate([order[i:i + 1, :] for i in range(folds)], axis=1)
-    order = jnp.where(order < SPILL, order, -1)
-    list_hot[...] = one_hot(order == lax.broadcasted_iota(jnp.int32, (PADDED, rows), 0))
     codes = jnp.concatenate([ids, slots] + [jnp.zeros_like(ids)] * 14, axis=0).astype(jnp.float32).astype(jnp.bfloat16)
-    codes = lax.dot_general(codes, list_hot[...], (((1,), (1,)), ((), ())), preferred_element_type=jnp.float32)
-    list_send[...] = matmul(list_hot[...], tok_ref[...]).astype(jnp.bfloat16)
-    list_send[SPILL:LIST, 0:PADDED] = codes.astype(jnp.bfloat16)
-    flag_src[...] = jnp.broadcast_to(jnp.maximum(jnp.sum(spills) - SPILL, 0.0), flag_src.shape)
+    excess = 0.0
+    for h in range(2):
+        column = (expert // 2 + h) % 2
+        spills = jnp.logical_and(far_spill, ids // 2 % 2 == column).astype(jnp.float32)
+        grid = jnp.concatenate([spills[:, i * lanes:(i + 1) * lanes] for i in range(folds)], axis=0)
+        marks = grid.astype(jnp.bfloat16)
+        order = matmul(marks, upto) + jnp.sum(matmul(before, marks), axis=1, keepdims=True)
+        order = jnp.where(grid > 0, order, 0.0).astype(jnp.int32) - 1
+        order = jnp.concatenate([order[i:i + 1, :] for i in range(folds)], axis=1)
+        order = jnp.where(order < SPILL, order, -1)
+        list_hot[h] = one_hot(order == lax.broadcasted_iota(jnp.int32, (PADDED, rows), 0))
+        named = lax.dot_general(codes, list_hot[h], (((1,), (1,)), ((), ())), preferred_element_type=jnp.float32)
+        list_send[h] = matmul(list_hot[h], tok_ref[...]).astype(jnp.bfloat16)
+        list_send[h, SPILL:LIST, 0:PADDED] = named.astype(jnp.bfloat16)
+        list_back[h, LIST:PADDED] = jnp.zeros((PADDED - LIST, width), jnp.bfloat16)
+        excess = jnp.maximum(excess, jnp.sum(spills) - SPILL)
+    flag_src[...] = jnp.broadcast_to(excess, flag_src.shape)
     for w in range(4):
         for i in range(2):
             lists[w, i, LIST:PADDED] = jnp.zeros((PADDED - LIST, width), jnp.bfloat16)
-    list_back[LIST:PADDED] = jnp.zeros((PADDED - LIST, width), jnp.bfloat16)
 
     pl.semaphore_wait(barrier, 16)
-    list_out().start()
+    list_out(0).start()
+    list_out(1).start()
 
     def flag_out(q, carry):
         flag_copy(q).start()
@@ -284,79 +287,60 @@
         z_hot[w, BASE:2 * BASE] = one_hot(flat_pos == target(3, w, BASE))
         z_hot[w, 2 * BASE:] = one_hot(flat_pos == target(1, w, slot_count))
         z_send[w] = matmul(z_hot[w], tok_ref[...]).astype(jnp.bfloat16)
-        for k in range(3):
-            z_copy(w, k).start()
-        return carry
-
-    lax.fori_loop(0, 1, z_pick, 0)
+        z_copy(w, 2).start()
+        return carry
+
     lax.fori_loop(0, 4, own_pick, 0)
-    lax.fori_loop(1, 4, z_pick, 0)
+    lax.fori_loop(0, 4, z_pick, 0)
     for load in loads:
         load.wait()
 
     def ffn(block):
         return expert_ffn(block, gate_w, up_w, down_w, hidden)
 
+    own_recv[0] = own_send[0]
+
     def own_step(w, carry):
         @pl.when(w > 0)
         def _():
             own_copy(w).wait_recv()
-            own_result[w] = ffn(own_recv[w])
+
+        own_result[w] = ffn(own_recv[w])
+
+        @pl.when(w > 0)
+        def _():
             own_return(w).start()
 
-        @pl.when(w == 0)
-        def _():
-            own_back[w] = ffn(own_send[w])
-
-        return carry
-
-    lax.fori_loop(0, 4, own_step, 0)
-
-    def flag_in(q, carry):
-        flag_copy(q).wait_recv()
-        return carry
-
-    lax.fori_loop(1, 16, flag_in, 0)
-    flags[0] = flag_src[...]
-    group_src[...] = jnp.max(flags[...], axis=0)
+        return carry
+
 
     me = node * 4 + expert
 
-    def round_step(r, carry):
-        @pl.when(r == 0)
-        def _():
-            for i in range(2):
-                arrived(0, i).wait_recv()
-
-                @pl.when(inner)
-                def _():
-                    forward_z(i).start()
-
-                forward_core(0, i).start()
-                forward_y(i).start()
-            flag_copy(1).wait_send()
-            group_copy().start()
-
-        @pl.when(r == 1)
-        def _():
-            for i in range(2):
-                arrived(2, i).wait_recv()
-                forward_core(2, i).start()
-
-        z_copy(r, 2).wait_recv()
-        near = slice(2 * BASE, 2 * BASE + slot_count)
-        far = slice(0, 2 * BASE)
-        z_result[r, near] = ffn(z_recv[r, near])
-        z_return(r, 2).start()
-        z_copy(r, 0).wait_recv()
-        z_copy(r, 1).wait_recv()
-        z_result[r, far] = ffn(z_recv[r, far])
-        z_return(r, 0).start()
-        z_return(r, 1).start()
-
-        w = (1 - r // 2) * (2 * r + 1) + (r // 2) * (6 - 2 * r)
-
-        @pl.when(w % 2 == 1)
+    near = slice(2 * BASE, 2 * BASE + slot_count)
+    far = slice(0, 2 * BASE)
+
+    def near_step(w, carry):
+        z_copy(w, 2).wait_recv()
+        z_result[w, near] = ffn(z_recv[w, near])
+
+        @pl.when(jnp.logical_not(inner))
+        def _():
+            z_return(w, 2).start()
+
+        return carry
+
+    def far_step(w, carry):
+        z_copy(w, 0).wait_recv()
+        z_copy(w, 1).wait_recv()
+        z_result[w, far] = ffn(z_recv[w, far])
+        z_return(w, 0).start()
+        z_return(w, 1).start()
+        return carry
+
+    def list_step(r, carry):
+        w = (1 - r // 2) * (2 * r + 1) + (r // 2) * (2 * r - 4)
+
+        @pl.when(r < 2)
         def _():
             for i in range(2):
                 arrived(w, i).wait_recv()
@@ -372,42 +356,96 @@
         for i in range(2):
             shares[w, i] = matmul_t(mine[i], y[i * BASE:(i + 1) * BASE]).astype(jnp.bfloat16)
 
-        @pl.when(w % 2 == 1)
+        @pl.when(r < 2)
         def _():
             for i in range(2):
                 share_core(w, i).start()
 
-        @pl.when(w == 2)
+        @pl.when(r >= 2)
         def _():
             for i in range(2):
-                share_core(3, i).wait_recv()
-                shares[2, i, 0:LIST] += core_in[1, i, 0:LIST]
-                share_y(i).start()
-
-        return carry
-
-    lax.fori_loop(0, 4, round_step, 0)
-
-    for i in range(2):
-        share_core(1, i).wait_recv()
-        share_y(i).wait_recv()
-        shares[0, i, 0:LIST] += core_in[0, i, 0:LIST] + y_in[i, 0:LIST]
-
-    @pl.when(jnp.logical_not(inner))
+                share_core(w + 1, i).wait_recv()
+                shares[w, i, 0:LIST] += core_in[w // 2, i, 0:LIST]
+
+                @pl.when(jnp.logical_not(inner))
+                def _():
+                    share_z(w, i).start()
+
+        return carry
+
+    def forward_lists():
+        for w in (0, 2):
+            for i in range(2):
+                arrived(w, i).wait_recv()
+
+                @pl.when(inner)
+                def _():
+                    forward_z(w, i).start()
+
+                forward_core(w, i).start()
+
+    def send_far():
+        for w in range(4):
+            for k in range(2):
+                z_copy(w, k).start()
+
+    def late_step(step, carry):
+        turn = step - 2 * (1 - kind)
+        lists_now = jnp.logical_and(turn >= 0, turn < 4)
+        w = jnp.where(lists_now, turn, jnp.where(turn < 0, step, step - 4))
+
+        @pl.when(jnp.logical_and(step == 2, jnp.logical_not(inner)))
+        def _():
+            forward_lists()
+
+        @pl.when(jnp.logical_and(step == 4, inner))
+        def _():
+            for i in range(4):
+                z_return(i, 2).start()
+
+        @pl.when(lists_now)
+        def _():
+            list_step(w, 0)
+
+        @pl.when(jnp.logical_not(lists_now))
+        def _():
+            far_step(w, 0)
+
+        return carry
+
+    lax.fori_loop(0, 4, own_step, 0)
+    own_back[0] = own_result[0]
+
+    @pl.when(inner)
     def _():
-        for i in range(2):
-            share_z(i).start()
+        forward_lists()
+
+    send_far()
+    lax.fori_loop(0, 4, near_step, 0)
+    lax.fori_loop(0, 8, late_step, 0)
+
+    @pl.when(inner)
+    def _():
+        for w in (0, 2):
+            for i in range(2):
+                share_z(w, 1 - i).wait_recv()
+                shares[w, i, 0:LIST] += z_in[w // 2, i, 0:LIST]
+                share_home(w, i).start()
+
+    def flag_in(q, carry):
+        flag_copy(q).wait_recv()
+        return carry
+
+    lax.fori_loop(1, 16, flag_in, 0)
+    flags[0] = flag_src[...]
+    group_src[...] = jnp.max(flags[...], axis=0)
+
+    flag_copy(1).wait_send()
+    group_copy().start()
 
     for w in range(1, 4):
         own_return(w).wait_recv()
     total[...] = matmul_t(own_hot[...].reshape(4 * slot_count, rows), own_back[...].reshape(4 * slot_count, width))
-
-    @pl.when(inner)
-    def _():
-        for i in range(2):
-            share_z(1 - i).wait_recv()
-            shares[0, i, 0:LIST] += z_in[i, 0:LIST]
-            share_home(i).start()
 
     def z_combine(w, carry):
         for k in (2, 0, 1):
@@ -416,8 +454,9 @@
         return carry
 
     lax.fori_loop(0, 4, z_combine, 0)
-    share_home(0).wait_recv()
-    total[...] += matmul_t(list_hot[...], list_back[...])
+    for h in range(2):
+        share_home(2 * h, 0).wait_recv()
+    total[...] += matmul_t(list_hot[...].reshape(2 * PADDED, rows), list_back[...].reshape(2 * PADDED, width))
     out_ref[...] = total[...].astype(out_ref.dtype)
 
     group_copy().wait_recv()
@@ -430,7 +469,6 @@
         for k in range(3):
             z_copy(w, k).wait_send()
             z_return(w, k).wait_send()
-    list_out().wait_send()
     group_copy().wait_send()
 
     def flag_sent(q, carry):
@@ -439,21 +477,19 @@
 
     lax.fori_loop(2, 16, flag_sent, 0)
     for i in range(2):
-        forward_y(i).wait_send()
-        forward_core(0, i).wait_send()
-        forward_core(2, i).wait_send()
-        share_core(1, i).wait_send()
-        share_core(3, i).wait_send()
-        share_y(i).wait_send()
-
-        @pl.when(inner)
-        def _():
-            forward_z(i).wait_send()
-            share_home(i).wait_send()
-
-        @pl.when(jnp.logical_not(inner))
-        def _():
-            share_z(i).wait_send()
+        list_out(i).wait_send()
+        for w in (0, 2):
+            forward_core(w, i).wait_send()
+            share_core(w + 1, i).wait_send()
+
+            @pl.when(inner)
+            def _():
+                forward_z(w, i).wait_send()
+                share_home(w, i).wait_send()
+
+            @pl.when(jnp.logical_not(inner))
+            def _():
+                share_z(w, i).wait_send()
 
 
 def solution(mesh):
@@ -504,10 +540,10 @@
             scratch_shapes=weights + [hidden, total]
             + [bf16(4, slot_count, rows)] + [bf16(*own)] * 4
             + [bf16(4, 2 * BASE + slot_count, rows)] + [bf16(*zed)] * 4
-            + [bf16(PADDED, rows), bf16(PADDED, width), bf16(4, 2, PADDED, width), bf16(4, 2, PADDED, width),
-               bf16(2, 2, PADDED, width), bf16(2, PADDED, width), bf16(2, PADDED, width), bf16(PADDED, width)]
+            + [bf16(2, PADDED, rows), bf16(2, PADDED, width), bf16(4, 2, PADDED, width), bf16(4, 2, PADDED, width),
+               bf16(2, 2, PADDED, width), bf16(2, 2, PADDED, width), bf16(2, PADDED, width)]
             + [flag, pltpu.VMEM((16, 8, 128), jnp.float32), flag, flag]
-            + [dma((3,)), dma((4, 4)), dma((4, 12)), dma((17,)), dma((17,)), dma((2, 16))],
+            + [dma((3,)), dma((4, 4)), dma((4, 12)), dma((18,)), dma((18,)), dma((2, 16))],
             compiler_params=params(0), name="packed_layer",
         )(*operands)
         return lax.cond(full[0, 0] > 0, lambda: scaled(padded()), lambda: scaled(picked))

time: 165 us -> 128 us (0.78)
  the two profiles are of different devices: /device:TPU:16 before, /device:TPU:11 now
where the time goes in v3:
time: 128 us; the launch traced here: 127 us
  Pallas kernels  125 us (98%)
  other arithmetic  1.47 us (1%)
    pallas_call x1, Pallas kernels, local_layer(): pl.pallas_call(functools.partial(packed_kernel, slot_count), out_shape=(p...  125 us

profile of v3, /device:TPU:11, one launch (start us, length us, event | category | flops | bytes accessed | tf_op | source)
XLA Modules:
  0.0 126.7 jit_solution(14327824594937821075)
XLA Ops:
  0.0 0.0 copy-start
  0.0 0.0 copy-start.1
  0.0 0.0 copy-start.2
  0.0 0.0 copy-start.3
  0.0 124.6 %packed_layer.1 = (bf16[1024,768]{1,0:T(8,128)(2,1)S(1)}, s32[1,1]{1,0:T(1,128)}) custom-call(bf16[1024,768]{1,0:T(8,128)(2,1)} %tok_ref.1, s32[1,1024]{1,0:T(1,128)} %bitcast.4, s32[1,1024]{1,0:T(1,128)} %bitcast.6, bf16[1,768,3072]{2,1,0:T(8,128)(2,1)} %gate_hbm.1, bf16[1,768,3072]{2,1,0:T(8,128)(2,1)} %up_hbm.1, bf16[1,3072,768]{2,1,0:T(8,128)(2,1)} %down_hbm.1), custom_call_target="tpu_custom_call" | custom-call | tf_op jit(solution)/shard_map/packed_layer/pallas_call | solution.py:536
  125.2 0.0 copy-done
  125.2 0.0 copy-done.1
  125.2 0.0 copy-done.2
  125.2 0.0 copy-done.3
  125.2 1.5 %fusion = bf16[1024,768]{1,0:T(8,128)(2,1)} fusion(bf16[1024,768]{1,0:T(8,128)(2,1)S(1)} %get-tuple-element.52, f32[1024]{0:T(1024)S(1)} %bitcast.8), kind=kLoop, calls=%fused_computation.1 | loop fusion | flops 2359296 | bytes 3149824 | tf_op jit(solution)/shard_map/cond/branch_0_fun/convert_element_type | solution.py:522
  (1 shorter events, 0.0 us)
Async XLA Ops:
  0.0 125.2 %copy-start = (bf16[1024,768]{1,0:T(8,128)(2,1)S(1)}, bf16[1024,768]{1,0:T(8,128)(2,1)}, u32[]{:S(2)}) copy-start(bf16[1024,768]{1,0:T(8,128)(2,1)} %tok_ref.1) | copy-start | bytes 4718596
  0.0 125.2 %copy-start.1 = (s32[1024,1]{0,1:T(1,128)S(1)}, s32[1024,1]{0,1:T(1,128)}, u32[]{:S(2)}) copy-start(s32[1024,1]{0,1:T(1,128)} %param.10) | copy-start | bytes 12292
  0.0 125.2 %copy-start.2 = (s32[1024,1]{0,1:T(1,128)S(1)}, s32[1024,1]{0,1:T(1,128)}, u32[]{:S(2)}) copy-start(s32[1024,1]{0,1:T(1,128)} %param.12) | copy-start | bytes 12292
  0.0 125.2 %copy-start.3 = (f32[1024,1]{0,1:T(1,128)S(1)}, f32[1024,1]{0,1:T(1,128)}, u32[]{:S(2)}) copy-start(f32[1024,1]{0,1:T(1,128)} %param.11) | copy-start | bytes 12292

commit v4 on v3

--- a/solution.py
+++ b/solution.py
@@ -11,10 +11,10 @@
 MESH = pl.DeviceIdType.MESH
 FF_TILE = 512
 REMOTE = 12
-BASE = 64
-SPILL = 144
-LIST = SPILL + 16
+BASE = 48
+SPILL = 160
 PADDED = 256
+CODES = 16
 
 
 def capacity(rows, top_k, experts):
@@ -47,12 +47,13 @@
 
 
 def expert_ffn(block, gate_w, up_w, down_w, hidden):
+    count = block.shape[0]
     for start in range(0, hidden.shape[1], FF_TILE):
         cols = slice(start, start + FF_TILE)
         gate = matmul(block, gate_w[:, cols])
         up = matmul(block, up_w[:, cols])
-        hidden[:, cols] = (jax.nn.silu(gate) * up).astype(jnp.bfloat16)
-    return matmul(hidden[...], down_w[...]).astype(jnp.bfloat16)
+        hidden[0:count, cols] = (jax.nn.silu(gate) * up).astype(jnp.bfloat16)
+    return matmul(hidden[0:count], down_w[...]).astype(jnp.bfloat16)
 
 
 def load_weights(refs, scratch, sems):
@@ -65,6 +66,23 @@
 def remote(src, dst, go, come, device):
     return pltpu.make_async_remote_copy(
         src_ref=src, dst_ref=dst, send_sem=go, recv_sem=come, device_id=device, device_id_type=MESH)
+
+
+class Both:
+    def __init__(self, first, second):
+        self.copies = (first, second)
+
+    def start(self):
+        for copy in self.copies:
+            copy.start()
+
+    def wait_send(self):
+        for copy in self.copies:
+            copy.wait_send()
+
+    def wait_recv(self):
+        for copy in self.copies:
+            copy.wait_recv()
 
 
 def padded_kernel(slot_count, tok_ref, ids_ref, slots_ref, gate_hbm, up_hbm, down_hbm, out_ref,
@@ -159,9 +177,9 @@
                   gate_w, up_w, down_w, hidden, total,
                   own_hot, own_send, own_recv, own_result, own_back,
                   z_hot, z_send, z_recv, z_result, z_back,
-                  list_hot, list_send, lists, shares, core_in, z_in, list_back,
+                  list_hot, list_send, lists, codes_out, codes_in, shares, core_in, z_in, list_back,
                   flag_src, flags, group_src, group_in,
-                  w_sem, own_sem, z_sem, list_sem, share_sem, flag_sem):
+                  w_sem, own_sem, z_sem, list_sem, code_sem, share_sem, flag_sem):
     rows, width = tok_ref.shape
     node, expert = lax.axis_index("node"), lax.axis_index("expert")
     inner = (node + 1) // 2 == 1
@@ -194,23 +212,27 @@
         return remote(z_result.at[w, z_part(k)], z_back.at[w, z_part(k)], z_sem.at[2, 3 * w + k], z_sem.at[3, 3 * w + k],
                       place((2, 3, 1)[k], w))
 
-    sent = pl.ds(0, LIST)
+    sent = pl.ds(0, SPILL)
     kind = 1 - ((node + 1) // 2 + 1) % 2
 
+    def list_copy(src, codes_src, at, go, device):
+        w, i = at
+        come = 2 * w + i
+        return Both(remote(src.at[sent], lists.at[w, i, sent], list_sem.at[go], list_sem.at[come], device),
+                    remote(codes_src, codes_in.at[w, i], code_sem.at[go], code_sem.at[come], device))
+
     def list_out(h):
-        return remote(list_send.at[h, sent], lists.at[2 * h, kind, sent], list_sem.at[8 + h], list_sem.at[4 * h + kind],
-                      {"node": 2 - node // 2, "expert": flip(expert, 2 * h)})
+        return list_copy(list_send.at[h], codes_out.at[h], (2 * h, kind), 8 + h,
+                         {"node": 2 - node // 2, "expert": flip(expert, 2 * h)})
 
     def arrived(w, i):
-        return remote(lists.at[w, i, sent], lists.at[w, i, sent], list_sem.at[8], list_sem.at[2 * w + i], place(0, 1))
+        return list_copy(lists.at[w, i], codes_in.at[w, i], (w, i), 8, place(0, 1))
 
     def forward_z(w, i):
-        return remote(lists.at[w, i, sent], lists.at[w, 1 - i, sent], list_sem.at[10 + w + i],
-                      list_sem.at[2 * w + 1 - i], place(1, 0))
+        return list_copy(lists.at[w, i], codes_in.at[w, i], (w, 1 - i), 10 + w + i, place(1, 0))
 
     def forward_core(w, i):
-        return remote(lists.at[w, i, sent], lists.at[w + 1, i, sent], list_sem.at[14 + w + i],
-                      list_sem.at[2 * w + 2 + i], place(0, 1))
+        return list_copy(lists.at[w, i], codes_in.at[w, i], (w + 1, i), 14 + w + i, place(0, 1))
 
     def share_core(w, i):
         return remote(shares.at[w, i, sent], core_in.at[w // 2, i, sent], share_sem.at[2 * w + i],
@@ -237,7 +259,7 @@
     folds = rows // lanes
     upto = one_hot(lax.broadcasted_iota(jnp.int32, (lanes, lanes), 0) <= lax.broadcasted_iota(jnp.int32, (lanes, lanes), 1))
     before = one_hot(lax.broadcasted_iota(jnp.int32, (folds, folds), 1) < lax.broadcasted_iota(jnp.int32, (folds, folds), 0))
-    codes = jnp.concatenate([ids, slots] + [jnp.zeros_like(ids)] * 14, axis=0).astype(jnp.float32).astype(jnp.bfloat16)
+    codes = jnp.concatenate([ids, slots] + [jnp.zeros_like(ids)] * (CODES - 2), axis=0).astype(jnp.float32).astype(jnp.bfloat16)
     excess = 0.0
     for h in range(2):
         column = (expert // 2 + h) % 2
@@ -251,13 +273,13 @@
         list_hot[h] = one_hot(order == lax.broadcasted_iota(jnp.int32, (PADDED, rows), 0))
         named = lax.dot_general(codes, list_hot[h], (((1,), (1,)), ((), ())), preferred_element_type=jnp.float32)
         list_send[h] = matmul(list_hot[h], tok_ref[...]).astype(jnp.bfloat16)
-        list_send[h, SPILL:LIST, 0:PADDED] = named.astype(jnp.bfloat16)
-        list_back[h, LIST:PADDED] = jnp.zeros((PADDED - LIST, width), jnp.bfloat16)
+        codes_out[h] = named.astype(jnp.bfloat16)
+        list_back[h, SPILL:PADDED] = jnp.zeros((PADDED - SPILL, width), jnp.bfloat16)
         excess = jnp.maximum(excess, jnp.sum(spills) - SPILL)
     flag_src[...] = jnp.broadcast_to(excess, flag_src.shape)
     for w in range(4):
         for i in range(2):
-            lists[w, i, LIST:PADDED] = jnp.zeros((PADDED - LIST, width), jnp.bfloat16)
+            lists[w, i, SPILL:PADDED] = jnp.zeros((PADDED - SPILL, width), jnp.bfloat16)
 
     pl.semaphore_wait(barrier, 16)
     list_out(0).start()
@@ -315,6 +337,7 @@
 
 
     me = node * 4 + expert
+    over = slot_count - BASE
 
     near = slice(2 * BASE, 2 * BASE + slot_count)
     far = slice(0, 2 * BASE)
@@ -322,11 +345,6 @@
     def near_step(w, carry):
         z_copy(w, 2).wait_recv()
         z_result[w, near] = ffn(z_recv[w, near])
-
-        @pl.when(jnp.logical_not(inner))
-        def _():
-            z_return(w, 2).start()
-
         return carry
 
     def far_step(w, carry):
@@ -338,34 +356,40 @@
         return carry
 
     def list_step(r, carry):
-        w = (1 - r // 2) * (2 * r + 1) + (r // 2) * (2 * r - 4)
-
-        @pl.when(r < 2)
-        def _():
+        w = r + 1 - 2 * (r % 2)
+
+        @pl.when(r % 2 == 0)
+        def _():
+            @pl.when(jnp.logical_not(inner))
+            def _():
+                for i in range(2):
+                    arrived(w - 1, i).wait_recv()
+                    forward_core(w - 1, i).start()
+
             for i in range(2):
                 arrived(w, i).wait_recv()
 
         mine, blocks = [], []
         for i in range(2):
-            codes = lists[w, i, SPILL:LIST, 0:PADDED].astype(jnp.float32)
-            slot = lax.broadcasted_iota(jnp.int32, (BASE, PADDED), 0) + BASE
+            codes = codes_in[w, i].astype(jnp.float32)
+            slot = lax.broadcasted_iota(jnp.int32, (over, PADDED), 0) + BASE
             hit = jnp.logical_and(codes[0:1].astype(jnp.int32) == me, codes[1:2].astype(jnp.int32) == slot)
             mine.append(one_hot(hit))
             blocks.append(matmul(mine[i], lists[w, i]).astype(jnp.bfloat16))
         y = ffn(jnp.concatenate(blocks, axis=0))
         for i in range(2):
-            shares[w, i] = matmul_t(mine[i], y[i * BASE:(i + 1) * BASE]).astype(jnp.bfloat16)
-
-        @pl.when(r < 2)
+            shares[w, i] = matmul_t(mine[i], y[i * over:(i + 1) * over]).astype(jnp.bfloat16)
+
+        @pl.when(r % 2 == 0)
         def _():
             for i in range(2):
                 share_core(w, i).start()
 
-        @pl.when(r >= 2)
+        @pl.when(r % 2 == 1)
         def _():
             for i in range(2):
                 share_core(w + 1, i).wait_recv()
-                shares[w, i, 0:LIST] += core_in[w // 2, i, 0:LIST]
+                shares[w, i, 0:SPILL] += core_in[w // 2, i, 0:SPILL]
 
                 @pl.when(jnp.logical_not(inner))
                 def _():
@@ -373,64 +397,88 @@
 
         return carry
 
-    def forward_lists():
-        for w in (0, 2):
-            for i in range(2):
-                arrived(w, i).wait_recv()
-
-                @pl.when(inner)
-                def _():
-                    forward_z(w, i).start()
-
-                forward_core(w, i).start()
-
-    def send_far():
+    def send_far(first):
         for w in range(4):
-            for k in range(2):
-                z_copy(w, k).start()
-
-    def late_step(step, carry):
-        turn = step - 2 * (1 - kind)
-        lists_now = jnp.logical_and(turn >= 0, turn < 4)
-        w = jnp.where(lists_now, turn, jnp.where(turn < 0, step, step - 4))
-
-        @pl.when(jnp.logical_and(step == 2, jnp.logical_not(inner)))
-        def _():
-            forward_lists()
-
-        @pl.when(jnp.logical_and(step == 4, inner))
-        def _():
-            for i in range(4):
-                z_return(i, 2).start()
-
-        @pl.when(lists_now)
-        def _():
-            list_step(w, 0)
-
-        @pl.when(jnp.logical_not(lists_now))
-        def _():
-            far_step(w, 0)
-
-        return carry
+            @pl.when(inner)
+            def _():
+                z_copy(w, first).start()
+
+            @pl.when(jnp.logical_not(inner))
+            def _():
+                z_copy(w, 1 - first).start()
 
     lax.fori_loop(0, 4, own_step, 0)
     own_back[0] = own_result[0]
-
-    @pl.when(inner)
-    def _():
-        forward_lists()
-
-    send_far()
-    lax.fori_loop(0, 4, near_step, 0)
-    lax.fori_loop(0, 8, late_step, 0)
 
     @pl.when(inner)
     def _():
         for w in (0, 2):
             for i in range(2):
-                share_z(w, 1 - i).wait_recv()
-                shares[w, i, 0:LIST] += z_in[w // 2, i, 0:LIST]
-                share_home(w, i).start()
+                arrived(w, i).wait_recv()
+                forward_core(w, i).start()
+                forward_z(w, i).start()
+
+    @pl.when(jnp.logical_not(inner))
+    def _():
+        send_far(1)
+
+    lax.fori_loop(0, 4, near_step, 0)
+
+    @pl.when(jnp.logical_not(inner))
+    def _():
+        send_far(0)
+
+    def merge_home(w):
+        for i in range(2):
+            share_z(w, 1 - i).wait_recv()
+            shares[w, i, 0:SPILL] += z_in[w // 2, i, 0:SPILL]
+            share_home(w, i).start()
+
+    def late_step(step, carry):
+        lists_now = step < 4
+
+        @pl.when(jnp.logical_and(step == 1, inner))
+        def _():
+            send_far(1)
+
+        @pl.when(jnp.logical_and(step == 3, inner))
+        def _():
+            send_far(0)
+
+        @pl.when(jnp.logical_and(step == 2, jnp.logical_not(inner)))
+        def _():
+            for w in range(2):
+                z_return(w, 2).start()
+
+        @pl.when(step == 4)
+        def _():
+            @pl.when(inner)
+            def _():
+                for w in range(2):
+                    z_return(w, 2).start()
+
+            for w in range(2, 4):
+                z_return(w, 2).start()
+
+        @pl.when(jnp.logical_and(step == 6, inner))
+        def _():
+            merge_home(0)
+
+        @pl.when(lists_now)
+        def _():
+            list_step(step, 0)
+
+        @pl.when(jnp.logical_not(lists_now))
+        def _():
+            far_step(step - 4, 0)
+
+        return carry
+
+    lax.fori_loop(0, 8, late_step, 0)
+
+    @pl.when(inner)
+    def _():
+        merge_home(2)
 
     def flag_in(q, carry):
         flag_copy(q).wait_recv()
@@ -507,7 +555,7 @@
         dma = pltpu.SemaphoreType.DMA
         weights = [pltpu.VMEM((width, ff), jnp.bfloat16), pltpu.VMEM((width, ff), jnp.bfloat16),
                    pltpu.VMEM((ff, width), jnp.bfloat16)]
-        hidden = pltpu.VMEM((slot_count, ff), jnp.bfloat16)
+        hidden = pltpu.VMEM((2 * (slot_count - BASE), ff), jnp.bfloat16)
         total = pltpu.VMEM((rows, width), jnp.float32)
         picked_shape = jax.ShapeDtypeStruct((rows, width), jnp.bfloat16)
         operands = (tokens, expert_ids.reshape(1, rows), slot_ids.reshape(1, rows), w_gate, w_up, w_down)
@@ -540,10 +588,11 @@
             scratch_shapes=weights + [hidden, total]
             + [bf16(4, slot_count, rows)] + [bf16(*own)] * 4
             + [bf16(4, 2 * BASE + slot_count, rows)] + [bf16(*zed)] * 4
-            + [bf16(2, PADDED, rows), bf16(2, PADDED, width), bf16(4, 2, PADDED, width), bf16(4, 2, PADDED, width),
+            + [bf16(2, PADDED, rows), bf16(2, PADDED, width), bf16(4, 2, PADDED, width),
+               bf16(2, CODES, PADDED), bf16(4, 2, CODES, PADDED), bf16(4, 2, PADDED, width),
                bf16(2, 2, PADDED, width), bf16(2, 2, PADDED, width), bf16(2, PADDED, width)]
             + [flag, pltpu.VMEM((16, 8, 128), jnp.float32), flag, flag]
-            + [dma((3,)), dma((4, 4)), dma((4, 12)), dma((18,)), dma((18,)), dma((2, 16))],
+            + [dma((3,)), dma((4, 4)), dma((4, 12)), dma((18,)), dma((18,)), dma((18,)), dma((2, 16))],
             compiler_params=params(0), name="packed_layer",
         )(*operands)
         return lax.cond(full[0, 0] > 0, lambda: scaled(padded()), lambda: scaled(picked))

time: 128 us -> 119 us (0.930)
  Pallas kernels: 125 us -> 116 us
    pallas_call x1, Pallas kernels: 125 us -> 116 us  [local_layer(): pl.pallas_call(functools.partial(packed_kernel, slot_count), out_shape=(p...]
where the time goes in v4:
time: 119 us
  Pallas kernels  116 us (97%)
  other arithmetic  1.47 us (1%)
    pallas_call x1, Pallas kernels, local_layer(): pl.pallas_call(functools.partial(packed_kernel, slot_count), out_shape=(p...  116 us

profile of v4, /device:TPU:11, one launch (start us, length us, event | category | flops | bytes accessed | tf_op | source)
XLA Modules:
  0.0 118.6 jit_solution(7033794728058351234)
XLA Ops:
  0.0 0.0 copy-start
  0.0 0.0 copy-start.1
  0.0 0.0 copy-start.2
  0.0 0.0 copy-start.3
  0.0 116.3 %packed_layer.1 = (bf16[1024,768]{1,0:T(8,128)(2,1)S(1)}, s32[1,1]{1,0:T(1,128)}) custom-call(bf16[1024,768]{1,0:T(8,128)(2,1)} %tok_ref.1, s32[1,1024]{1,0:T(1,128)} %bitcast.4, s32[1,1024]{1,0:T(1,128)} %bitcast.6, bf16[1,768,3072]{2,1,0:T(8,128)(2,1)} %gate_hbm.1, bf16[1,768,3072]{2,1,0:T(8,128)(2,1)} %up_hbm.1, bf16[1,3072,768]{2,1,0:T(8,128)(2,1)} %down_hbm.1), custom_call_target="tpu_custom_call" | custom-call | tf_op jit(solution)/shard_map/packed_layer/pallas_call | solution.py:584
  116.8 0.0 copy-done
  116.9 0.0 copy-done.1
  116.9 0.0 copy-done.2
  116.9 0.0 copy-done.3
  116.9 0.2 conditional.2
  117.1 1.5 %fusion = bf16[1024,768]{1,0:T(8,128)(2,1)} fusion(bf16[1024,768]{1,0:T(8,128)(2,1)S(1)} %get-tuple-element.52, f32[1024]{0:T(1024)S(1)} %bitcast.8), kind=kLoop, calls=%fused_computation.1 | loop fusion | flops 2359296 | bytes 3149824 | tf_op jit(solution)/shard_map/cond/branch_0_fun/convert_element_type | solution.py:570
Async XLA Ops:
  0.0 116.8 %copy-start = (bf16[1024,768]{1,0:T(8,128)(2,1)S(1)}, bf16[1024,768]{1,0:T(8,128)(2,1)}, u32[]{:S(2)}) copy-start(bf16[1024,768]{1,0:T(8,128)(2,1)} %tok_ref.1) | copy-start | bytes 4718596
  0.0 116.9 %copy-start.1 = (s32[1024,1]{0,1:T(1,128)S(1)}, s32[1024,1]{0,1:T(1,128)}, u32[]{:S(2)}) copy-start(s32[1024,1]{0,1:T(1,128)} %param.10) | copy-start | bytes 12292
  0.0 116.9 %copy-start.2 = (s32[1024,1]{0,1:T(1,128)S(1)}, s32[1024,1]{0,1:T(1,128)}, u32[]{:S(2)}) copy-start(s32[1024,1]{0,1:T(1,128)} %param.12) | copy-start | bytes 12292
  0.0 116.9 %copy-start.3 = (f32[1024,1]{0,1:T(1,128)S(1)}, f32[1024,1]{0,1:T(1,128)}, u32[]{:S(2)}) copy-start(f32[1024,1]{0,1:T(1,128)} %param.11) | copy-start | bytes 12292

commit v5 on v4

--- a/solution.py
+++ b/solution.py
@@ -15,6 +15,11 @@
 SPILL = 160
 PADDED = 256
 CODES = 16
+INNER = dict(order="oooollllffffnnnn", near=(0, 0, 0, 0), to_inner=(5, 5, 6, 6), to_outer=(6, 6, 7, 7),
+             near_back=(14, 15, 16, 16), home=(11, 16), lists=((0, 0, 4), (0, 1, 4), (2, 0, 4), (2, 1, 4)))
+OUTER = dict(order="oooonnnnllllffff", near=(0, 0, 0, 0), to_inner=(4, 4, 4, 4), to_outer=(8, 8, 8, 8),
+             near_back=(10, 10, 13, 13))
+KINDS = "onfl"
 
 
 def capacity(rows, top_k, experts):
@@ -183,6 +188,7 @@
     rows, width = tok_ref.shape
     node, expert = lax.axis_index("node"), lax.axis_index("expert")
     inner = (node + 1) // 2 == 1
+    roles = ((INNER, inner), (OUTER, jnp.logical_not(inner)))
     loads = load_weights((gate_hbm, up_hbm, down_hbm), (gate_w, up_w, down_w), w_sem)
 
     barrier = pltpu.get_barrier_semaphore()
@@ -309,7 +315,14 @@
         z_hot[w, BASE:2 * BASE] = one_hot(flat_pos == target(3, w, BASE))
         z_hot[w, 2 * BASE:] = one_hot(flat_pos == target(1, w, slot_count))
         z_send[w] = matmul(z_hot[w], tok_ref[...]).astype(jnp.bfloat16)
-        z_copy(w, 2).start()
+
+        for role, is_role in roles:
+            early = [v for v in range(4) if role["near"][v] == 0]
+            if early == [0, 1, 2, 3]:
+                @pl.when(is_role)
+                def _():
+                    z_copy(w, 2).start()
+
         return carry
 
     lax.fori_loop(0, 4, own_pick, 0)
@@ -397,36 +410,10 @@
 
         return carry
 
-    def send_far(first):
-        for w in range(4):
-            @pl.when(inner)
-            def _():
-                z_copy(w, first).start()
-
-            @pl.when(jnp.logical_not(inner))
-            def _():
-                z_copy(w, 1 - first).start()
-
-    lax.fori_loop(0, 4, own_step, 0)
-    own_back[0] = own_result[0]
-
-    @pl.when(inner)
-    def _():
-        for w in (0, 2):
-            for i in range(2):
-                arrived(w, i).wait_recv()
-                forward_core(w, i).start()
-                forward_z(w, i).start()
-
-    @pl.when(jnp.logical_not(inner))
-    def _():
-        send_far(1)
-
-    lax.fori_loop(0, 4, near_step, 0)
-
-    @pl.when(jnp.logical_not(inner))
-    def _():
-        send_far(0)
+    def forward_list(w, i):
+        arrived(w, i).wait_recv()
+        forward_core(w, i).start()
+        forward_z(w, i).start()
 
     def merge_home(w):
         for i in range(2):
@@ -434,51 +421,62 @@
             shares[w, i, 0:SPILL] += z_in[w // 2, i, 0:SPILL]
             share_home(w, i).start()
 
-    def late_step(step, carry):
-        lists_now = step < 4
-
-        @pl.when(jnp.logical_and(step == 1, inner))
-        def _():
-            send_far(1)
-
-        @pl.when(jnp.logical_and(step == 3, inner))
-        def _():
-            send_far(0)
-
-        @pl.when(jnp.logical_and(step == 2, jnp.logical_not(inner)))
-        def _():
-            for w in range(2):
-                z_return(w, 2).start()
-
-        @pl.when(step == 4)
-        def _():
-            @pl.when(inner)
+    def acts(role, slot):
+        same = kind_of_far[role is INNER]
+        found = []
+        for w in range(4):
+            if role["near"][w] == slot and role["near"] != (0, 0, 0, 0):
+                found.append(z_copy(w, 2).start)
+        for name, k in (("to_inner", same), ("to_outer", 1 - same)):
+            found += [z_copy(w, k).start for w in range(4) if role[name][w] == slot]
+        found += [z_return(w, 2).start for w in range(4) if role["near_back"][w] == slot]
+        if role is INNER:
+            found += [functools.partial(forward_list, w, i) for w, i, when in role["lists"] if when == slot]
+            found += [functools.partial(merge_home, w) for w in (0, 2) if role["home"][w // 2] == slot]
+        return found
+
+    kind_of_far = {True: 1, False: 0}
+
+    def fire(at):
+        for role, is_role in roles:
+            for slot in range(len(role["order"])):
+                todo = acts(role, slot)
+                if todo:
+                    @pl.when(jnp.logical_and(at == slot, is_role))
+                    def _():
+                        for act in todo:
+                            act()
+
+    def table(values, at):
+        inner_values, outer_values = values
+        total = 0
+        for slot, (a, b) in enumerate(zip(inner_values, outer_values)):
+            total = total + jnp.where(at == slot, a if a == b else jnp.where(inner, a, b), 0)
+        return total
+
+    orders = [role["order"] for role, _ in roles]
+    sorts = [[KINDS.index(letter) for letter in order] for order in orders]
+    turns = [[order[:slot].count(letter) for slot, letter in enumerate(order)] for order in orders]
+
+    def slot_step(at, carry):
+        fire(at)
+        sort, turn = table(sorts, at), table(turns, at)
+        for number, step in enumerate((own_step, near_step, far_step, list_step)):
+            @pl.when(sort == number)
             def _():
-                for w in range(2):
-                    z_return(w, 2).start()
-
-            for w in range(2, 4):
-                z_return(w, 2).start()
-
-        @pl.when(jnp.logical_and(step == 6, inner))
-        def _():
-            merge_home(0)
-
-        @pl.when(lists_now)
-        def _():
-            list_step(step, 0)
-
-        @pl.when(jnp.logical_not(lists_now))
-        def _():
-            far_step(step - 4, 0)
-
-        return carry
-
-    lax.fori_loop(0, 8, late_step, 0)
-
-    @pl.when(inner)
-    def _():
-        merge_home(2)
+                step(turn, 0)
+
+        return carry
+
+    lax.fori_loop(0, 16, slot_step, 0)
+    own_back[0] = own_result[0]
+    for role, is_role in roles:
+        todo = acts(role, 16)
+        if todo:
+            @pl.when(is_role)
+            def _():
+                for act in todo:
+                    act()
 
     def flag_in(q, carry):
         flag_copy(q).wait_recv()

time: 119 us -> 115 us (0.966)
  Pallas kernels: 116 us -> 112 us
    pallas_call x1, Pallas kernels: 116 us -> 112 us  [local_layer(): pl.pallas_call(functools.partial(packed_kernel, slot_count), out_shape=(p...]
where the time goes in v5:
time: 115 us; the launch traced here: 114 us
  Pallas kernels  112 us (97%)
  other arithmetic  1.47 us (1%)
    pallas_call x1, Pallas kernels, local_layer(): pl.pallas_call(functools.partial(packed_kernel, slot_count), out_shape=(p...  112 us

profile of v5, /device:TPU:11, one launch (start us, length us, event | category | flops | bytes accessed | tf_op | source)
XLA Modules:
  0.0 114.0 jit_solution(1974940653543179039)
XLA Ops:
  0.0 0.0 copy-start
  0.0 0.0 copy-start.1
  0.0 0.0 copy-start.2
  0.0 0.0 copy-start.3
  0.0 111.8 %packed_layer.1 = (bf16[1024,768]{1,0:T(8,128)(2,1)S(1)}, s32[1,1]{1,0:T(1,128)}) custom-call(bf16[1024,768]{1,0:T(8,128)(2,1)} %tok_ref.1, s32[1,1024]{1,0:T(1,128)} %bitcast.4, s32[1,1024]{1,0:T(1,128)} %bitcast.6, bf16[1,768,3072]{2,1,0:T(8,128)(2,1)} %gate_hbm.1, bf16[1,768,3072]{2,1,0:T(8,128)(2,1)} %up_hbm.1, bf16[1,3072,768]{2,1,0:T(8,128)(2,1)} %down_hbm.1), custom_call_target="tpu_custom_call" | custom-call | tf_op jit(solution)/shard_map/packed_layer/pallas_call | solution.py:582
  112.4 0.0 copy-done
  112.4 0.0 copy-done.1
  112.5 0.0 copy-done.2
  112.5 0.0 copy-done.3
  112.5 1.5 %fusion = bf16[1024,768]{1,0:T(8,128)(2,1)} fusion(bf16[1024,768]{1,0:T(8,128)(2,1)S(1)} %get-tuple-element.52, f32[1024]{0:T(1024)S(1)} %bitcast.8), kind=kLoop, calls=%fused_computation.1 | loop fusion | flops 2359296 | bytes 3149824 | tf_op jit(solution)/shard_map/cond/branch_0_fun/convert_element_type | solution.py:568
  (1 shorter events, 0.0 us)
Async XLA Ops:
  0.0 112.4 %copy-start = (bf16[1024,768]{1,0:T(8,128)(2,1)S(1)}, bf16[1024,768]{1,0:T(8,128)(2,1)}, u32[]{:S(2)}) copy-start(bf16[1024,768]{1,0:T(8,128)(2,1)} %tok_ref.1) | copy-start | bytes 4718596
  0.0 112.4 %copy-start.1 = (s32[1024,1]{0,1:T(1,128)S(1)}, s32[1024,1]{0,1:T(1,128)}, u32[]{:S(2)}) copy-start(s32[1024,1]{0,1:T(1,128)} %param.10) | copy-start | bytes 12292
  0.0 112.5 %copy-start.2 = (s32[1024,1]{0,1:T(1,128)S(1)}, s32[1024,1]{0,1:T(1,128)}, u32[]{:S(2)}) copy-start(s32[1024,1]{0,1:T(1,128)} %param.12) | copy-start | bytes 12292
  0.0 112.5 %copy-start.3 = (f32[1024,1]{0,1:T(1,128)S(1)}, f32[1024,1]{0,1:T(1,128)}, u32[]{:S(2)}) copy-start(f32[1024,1]{0,1:T(1,128)} %param.11) | copy-start | bytes 12292

commit v6 on v5

--- a/solution.py
+++ b/solution.py
@@ -15,8 +15,8 @@
 SPILL = 160
 PADDED = 256
 CODES = 16
-INNER = dict(order="oooollllffffnnnn", near=(0, 0, 0, 0), to_inner=(5, 5, 6, 6), to_outer=(6, 6, 7, 7),
-             near_back=(14, 15, 16, 16), home=(11, 16), lists=((0, 0, 4), (0, 1, 4), (2, 0, 4), (2, 1, 4)))
+INNER = dict(order="oolollloffffnnnn", near=(0, 0, 0, 0), to_inner=(3, 3, 4, 4), to_outer=(5, 5, 6, 6),
+             near_back=(14, 15, 16, 16), home=(12, 16), lists=((0, 0, 2), (0, 1, 2), (2, 0, 2), (2, 1, 2)))
 OUTER = dict(order="oooonnnnllllffff", near=(0, 0, 0, 0), to_inner=(4, 4, 4, 4), to_outer=(8, 8, 8, 8),
              near_back=(10, 10, 13, 13))
 KINDS = "onfl"
@@ -224,8 +224,9 @@
     def list_copy(src, codes_src, at, go, device):
         w, i = at
         come = 2 * w + i
+        named = pl.ds(0, 2)
         return Both(remote(src.at[sent], lists.at[w, i, sent], list_sem.at[go], list_sem.at[come], device),
-                    remote(codes_src, codes_in.at[w, i], code_sem.at[go], code_sem.at[come], device))
+                    remote(codes_src.at[named], codes_in.at[w, i, named], code_sem.at[go], code_sem.at[come], device))
 
     def list_out(h):
         return list_copy(list_send.at[h], codes_out.at[h], (2 * h, kind), 8 + h,
@@ -253,10 +254,10 @@
                       share_sem.at[16 + w // 2], place(2 + i, w))
 
     def flag_copy(q):
-        return remote(flag_src, flags.at[q], flag_sem.at[0, q], flag_sem.at[1, q], place(q // 4, q % 4))
+        return remote(flag_src.at[pl.ds(0, 1)], flags.at[q, pl.ds(0, 1)], flag_sem.at[0, q], flag_sem.at[1, q], place(q // 4, q % 4))
 
     def group_copy():
-        return remote(group_src, group_in, flag_sem.at[0, 0], flag_sem.at[1, 0], twin)
+        return remote(group_src.at[pl.ds(0, 1)], group_in.at[pl.ds(0, 1)], flag_sem.at[0, 0], flag_sem.at[1, 0], twin)
 
     ids, slots = ids_ref[...], slots_ref[...]
     flat_pos = jnp.where(slots >= 0, ids * slot_count + slots, 16 * slot_count)
@@ -279,7 +280,7 @@
         list_hot[h] = one_hot(order == lax.broadcasted_iota(jnp.int32, (PADDED, rows), 0))
         named = lax.dot_general(codes, list_hot[h], (((1,), (1,)), ((), ())), preferred_element_type=jnp.float32)
         list_send[h] = matmul(list_hot[h], tok_ref[...]).astype(jnp.bfloat16)
-        codes_out[h] = named.astype(jnp.bfloat16)
+        codes_out[h] = named[0:8]
         list_back[h, SPILL:PADDED] = jnp.zeros((PADDED - SPILL, width), jnp.bfloat16)
         excess = jnp.maximum(excess, jnp.sum(spills) - SPILL)
     flag_src[...] = jnp.broadcast_to(excess, flag_src.shape)
@@ -287,28 +288,27 @@
         for i in range(2):
             lists[w, i, SPILL:PADDED] = jnp.zeros((PADDED - SPILL, width), jnp.bfloat16)
 
+    def target(by_node, w, count):
+        return lax.broadcasted_iota(jnp.int32, (count, rows), 0) + expert_of(by_node, w) * slot_count
+
+    def own_pick(w, carry):
+        own_hot[w] = one_hot(flat_pos == target(0, w, slot_count))
+        own_send[w] = matmul(own_hot[w], tok_ref[...]).astype(jnp.bfloat16)
+
+        return carry
+
+    lax.fori_loop(0, 4, own_pick, 0)
     pl.semaphore_wait(barrier, 16)
     list_out(0).start()
     list_out(1).start()
+    for w in (2, 3, 1):
+        own_copy(w).start()
 
     def flag_out(q, carry):
         flag_copy(q).start()
         return carry
 
     lax.fori_loop(1, 16, flag_out, 0)
-
-    def target(by_node, w, count):
-        return lax.broadcasted_iota(jnp.int32, (count, rows), 0) + expert_of(by_node, w) * slot_count
-
-    def own_pick(w, carry):
-        own_hot[w] = one_hot(flat_pos == target(0, w, slot_count))
-        own_send[w] = matmul(own_hot[w], tok_ref[...]).astype(jnp.bfloat16)
-
-        @pl.when(w > 0)
-        def _():
-            own_copy(w).start()
-
-        return carry
 
     def z_pick(w, carry):
         z_hot[w, 0:BASE] = one_hot(flat_pos == target(2, w, BASE))
@@ -325,7 +325,6 @@
 
         return carry
 
-    lax.fori_loop(0, 4, own_pick, 0)
     lax.fori_loop(0, 4, z_pick, 0)
     for load in loads:
         load.wait()
@@ -384,7 +383,7 @@
 
         mine, blocks = [], []
         for i in range(2):
-            codes = codes_in[w, i].astype(jnp.float32)
+            codes = codes_in[w, i]
             slot = lax.broadcasted_iota(jnp.int32, (over, PADDED), 0) + BASE
             hit = jnp.logical_and(codes[0:1].astype(jnp.int32) == me, codes[1:2].astype(jnp.int32) == slot)
             mine.append(one_hot(hit))
@@ -484,7 +483,7 @@
 
     lax.fori_loop(1, 16, flag_in, 0)
     flags[0] = flag_src[...]
-    group_src[...] = jnp.max(flags[...], axis=0)
+    group_src[0:1] = jnp.max(flags[:, 0:1], axis=0)
 
     flag_copy(1).wait_send()
     group_copy().start()
@@ -500,13 +499,13 @@
         return carry
 
     lax.fori_loop(0, 4, z_combine, 0)
-    for h in range(2):
-        share_home(2 * h, 0).wait_recv()
-    total[...] += matmul_t(list_hot[...].reshape(2 * PADDED, rows), list_back[...].reshape(2 * PADDED, width))
-    out_ref[...] = total[...].astype(out_ref.dtype)
+    share_home(0, 0).wait_recv()
+    total[...] += matmul_t(list_hot[0], list_back[0])
+    share_home(2, 0).wait_recv()
+    out_ref[...] = (total[...] + matmul_t(list_hot[1], list_back[1])).astype(out_ref.dtype)
 
     group_copy().wait_recv()
-    full_ref[0, 0] = (jnp.max(jnp.maximum(group_src[...], group_in[...])) > 0.0).astype(jnp.int32)
+    full_ref[0, 0] = (jnp.max(jnp.maximum(group_src[0:1], group_in[0:1])) > 0.0).astype(jnp.int32)
 
     for w in range(1, 4):
         own_copy(w).wait_send()
@@ -587,7 +586,7 @@
             + [bf16(4, slot_count, rows)] + [bf16(*own)] * 4
             + [bf16(4, 2 * BASE + slot_count, rows)] + [bf16(*zed)] * 4
             + [bf16(2, PADDED, rows), bf16(2, PADDED, width), bf16(4, 2, PADDED, width),
-               bf16(2, CODES, PADDED), bf16(4, 2, CODES, PADDED), bf16(4, 2, PADDED, width),
+               pltpu.VMEM((2, 8, PADDED), jnp.float32), pltpu.VMEM((4, 2, 8, PADDED), jnp.float32), bf16(4, 2, PADDED, width),
                bf16(2, 2, PADDED, width), bf16(2, 2, PADDED, width), bf16(2, PADDED, width)]
             + [flag, pltpu.VMEM((16, 8, 128), jnp.float32), flag, flag]
             + [dma((3,)), dma((4, 4)), dma((4, 12)), dma((18,)), dma((18,)), dma((18,)), dma((2, 16))],

time: 115 us -> 113 us (0.983)
  the two profiles are of different devices: /device:TPU:11 before, /device:TPU:1 now
where the time goes in v6:
time: 113 us
  Pallas kernels  110 us (97%)
  other arithmetic  1.47 us (1%)
    pallas_call x1, Pallas kernels, local_layer(): pl.pallas_call(functools.partial(packed_kernel, slot_count), out_shape=(p...  110 us

profile of v6, /device:TPU:1, one launch (start us, length us, event | category | flops | bytes accessed | tf_op | source)
XLA Modules:
  0.0 112.6 jit_solution(3447893789654617000)
XLA Ops:
  0.0 0.0 copy-start
  0.0 0.0 copy-start.1
  0.0 0.0 copy-start.2
  0.0 0.0 copy-start.3
  0.0 110.5 %packed_layer.1 = (bf16[1024,768]{1,0:T(8,128)(2,1)S(1)}, s32[1,1]{1,0:T(1,128)}) custom-call(bf16[1024,768]{1,0:T(8,128)(2,1)} %tok_ref.1, s32[1,1024]{1,0:T(1,128)} %bitcast.4, s32[1,1024]{1,0:T(1,128)} %bitcast.6, bf16[1,768,3072]{2,1,0:T(8,128)(2,1)} %gate_hbm.1, bf16[1,768,3072]{2,1,0:T(8,128)(2,1)} %up_hbm.1, bf16[1,3072,768]{2,1,0:T(8,128)(2,1)} %down_hbm.1), custom_call_target="tpu_custom_call" | custom-call | tf_op jit(solution)/shard_map/packed_layer/pallas_call | solution.py:581
  111.0 0.0 copy-done
  111.1 0.0 copy-done.1
  111.1 0.0 copy-done.2
  111.1 0.0 copy-done.3
  111.1 1.5 %fusion = bf16[1024,768]{1,0:T(8,128)(2,1)} fusion(bf16[1024,768]{1,0:T(8,128)(2,1)S(1)} %get-tuple-element.52, f32[1024]{0:T(1024)S(1)} %bitcast.8), kind=kLoop, calls=%fused_computation.1 | loop fusion | flops 2359296 | bytes 3149824 | tf_op jit(solution)/shard_map/cond/branch_0_fun/convert_element_type | solution.py:567
  (1 shorter events, 0.0 us)
Async XLA Ops:
  0.0 111.0 %copy-start = (bf16[1024,768]{1,0:T(8,128)(2,1)S(1)}, bf16[1024,768]{1,0:T(8,128)(2,1)}, u32[]{:S(2)}) copy-start(bf16[1024,768]{1,0:T(8,128)(2,1)} %tok_ref.1) | copy-start | bytes 4718596
  0.0 111.1 %copy-start.1 = (s32[1024,1]{0,1:T(1,128)S(1)}, s32[1024,1]{0,1:T(1,128)}, u32[]{:S(2)}) copy-start(s32[1024,1]{0,1:T(1,128)} %param.10) | copy-start | bytes 12292
  0.0 111.1 %copy-start.2 = (s32[1024,1]{0,1:T(1,128)S(1)}, s32[1024,1]{0,1:T(1,128)}, u32[]{:S(2)}) copy-start(s32[1024,1]{0,1:T(1,128)} %param.12) | copy-start | bytes 12292
  0.0 111.1 %copy-start.3 = (f32[1024,1]{0,1:T(1,128)S(1)}, f32[1024,1]{0,1:T(1,128)}, u32[]{:S(2)}) copy-start(f32[1024,1]{0,1:T(1,128)} %param.11) | copy-start | bytes 12292

commit v7 on v6

--- a/solution.py
+++ b/solution.py
@@ -15,8 +15,8 @@
 SPILL = 160
 PADDED = 256
 CODES = 16
-INNER = dict(order="oolollloffffnnnn", near=(0, 0, 0, 0), to_inner=(3, 3, 4, 4), to_outer=(5, 5, 6, 6),
-             near_back=(14, 15, 16, 16), home=(12, 16), lists=((0, 0, 2), (0, 1, 2), (2, 0, 2), (2, 1, 2)))
+INNER = dict(order="oollolloffffnnnn", near=(0, 0, 0, 0), to_inner=(5, 5, 6, 6), to_outer=(6, 6, 7, 7),
+             near_back=(14, 15, 16, 16), home=(13, 16), lists=((0, 0, 2), (2, 0, 2), (0, 1, 5), (2, 1, 5)))
 OUTER = dict(order="oooonnnnllllffff", near=(0, 0, 0, 0), to_inner=(4, 4, 4, 4), to_outer=(8, 8, 8, 8),
              near_back=(10, 10, 13, 13))
 KINDS = "onfl"
@@ -189,8 +189,6 @@
     node, expert = lax.axis_index("node"), lax.axis_index("expert")
     inner = (node + 1) // 2 == 1
     roles = ((INNER, inner), (OUTER, jnp.logical_not(inner)))
-    loads = load_weights((gate_hbm, up_hbm, down_hbm), (gate_w, up_w, down_w), w_sem)
-
     barrier = pltpu.get_barrier_semaphore()
     twin = {"data": (lax.axis_index("data") + 1) % 2}
     pl.semaphore_signal(barrier, inc=1, device_id=twin, device_id_type=MESH)
@@ -200,6 +198,7 @@
         return carry
 
     lax.fori_loop(1, 16, greet, 0)
+    loads = load_weights((gate_hbm, up_hbm, down_hbm), (gate_w, up_w, down_w), w_sem)
 
     def own_copy(w):
         return remote(own_send.at[w], own_recv.at[w], own_sem.at[0, w], own_sem.at[1, w], place(0, w))
@@ -279,14 +278,11 @@
         order = jnp.where(order < SPILL, order, -1)
         list_hot[h] = one_hot(order == lax.broadcasted_iota(jnp.int32, (PADDED, rows), 0))
         named = lax.dot_general(codes, list_hot[h], (((1,), (1,)), ((), ())), preferred_element_type=jnp.float32)
-        list_send[h] = matmul(list_hot[h], tok_ref[...]).astype(jnp.bfloat16)
+        list_send[h, 0:SPILL] = matmul(list_hot[h, 0:SPILL], tok_ref[...]).astype(jnp.bfloat16)
         codes_out[h] = named[0:8]
         list_back[h, SPILL:PADDED] = jnp.zeros((PADDED - SPILL, width), jnp.bfloat16)
         excess = jnp.maximum(excess, jnp.sum(spills) - SPILL)
     flag_src[...] = jnp.broadcast_to(excess, flag_src.shape)
-    for w in range(4):
-        for i in range(2):
-            lists[w, i, SPILL:PADDED] = jnp.zeros((PADDED - SPILL, width), jnp.bfloat16)
 
     def target(by_node, w, count):
         return lax.broadcasted_iota(jnp.int32, (count, rows), 0) + expert_of(by_node, w) * slot_count
@@ -326,6 +322,9 @@
         return carry
 
     lax.fori_loop(0, 4, z_pick, 0)
+    for w in range(4):
+        for i in range(2):
+            lists[w, i, SPILL:PADDED] = jnp.zeros((PADDED - SPILL, width), jnp.bfloat16)
     for load in loads:
         load.wait()
 
@@ -368,38 +367,40 @@
         return carry
 
     def list_step(r, carry):
-        w = r + 1 - 2 * (r % 2)
-
-        @pl.when(r % 2 == 0)
+        i = 1 - kind + (r // 2) * (2 * kind - 1)
+        odd = 1 - r % 2
+
+        @pl.when(odd == 1)
         def _():
             @pl.when(jnp.logical_not(inner))
             def _():
-                for i in range(2):
-                    arrived(w - 1, i).wait_recv()
-                    forward_core(w - 1, i).start()
-
-            for i in range(2):
+                for w in (0, 2):
+                    arrived(w, i).wait_recv()
+                    forward_core(w, i).start()
+
+            for w in (1, 3):
                 arrived(w, i).wait_recv()
 
         mine, blocks = [], []
-        for i in range(2):
+        for h in range(2):
+            w = 2 * h + odd
             codes = codes_in[w, i]
             slot = lax.broadcasted_iota(jnp.int32, (over, PADDED), 0) + BASE
             hit = jnp.logical_and(codes[0:1].astype(jnp.int32) == me, codes[1:2].astype(jnp.int32) == slot)
             mine.append(one_hot(hit))
-            blocks.append(matmul(mine[i], lists[w, i]).astype(jnp.bfloat16))
+            blocks.append(matmul(mine[h], lists[w, i]).astype(jnp.bfloat16))
         y = ffn(jnp.concatenate(blocks, axis=0))
-        for i in range(2):
-            shares[w, i] = matmul_t(mine[i], y[i * over:(i + 1) * over]).astype(jnp.bfloat16)
-
-        @pl.when(r % 2 == 0)
-        def _():
-            for i in range(2):
+        for h in range(2):
+            shares[2 * h + odd, i] = matmul_t(mine[h], y[h * over:(h + 1) * over]).astype(jnp.bfloat16)
+
+        @pl.when(odd == 1)
+        def _():
+            for w in (1, 3):
                 share_core(w, i).start()
 
-        @pl.when(r % 2 == 1)
-        def _():
-            for i in range(2):
+        @pl.when(odd == 0)
+        def _():
+            for w in (0, 2):
                 share_core(w + 1, i).wait_recv()
                 shares[w, i, 0:SPILL] += core_in[w // 2, i, 0:SPILL]
 
@@ -414,8 +415,8 @@
         forward_core(w, i).start()
         forward_z(w, i).start()
 
-    def merge_home(w):
-        for i in range(2):
+    def merge_home(i):
+        for w in (0, 2):
             share_z(w, 1 - i).wait_recv()
             shares[w, i, 0:SPILL] += z_in[w // 2, i, 0:SPILL]
             share_home(w, i).start()
@@ -431,7 +432,7 @@
         found += [z_return(w, 2).start for w in range(4) if role["near_back"][w] == slot]
         if role is INNER:
             found += [functools.partial(forward_list, w, i) for w, i, when in role["lists"] if when == slot]
-            found += [functools.partial(merge_home, w) for w in (0, 2) if role["home"][w // 2] == slot]
+            found += [functools.partial(merge_home, i) for i in (0, 1) if role["home"][i] == slot]
         return found
 
     kind_of_far = {True: 1, False: 0}
@@ -499,11 +500,6 @@
         return carry
 
     lax.fori_loop(0, 4, z_combine, 0)
-    share_home(0, 0).wait_recv()
-    total[...] += matmul_t(list_hot[0], list_back[0])
-    share_home(2, 0).wait_recv()
-    out_ref[...] = (total[...] + matmul_t(list_hot[1], list_back[1])).astype(out_ref.dtype)
-
     group_copy().wait_recv()
     full_ref[0, 0] = (jnp.max(jnp.maximum(group_src[0:1], group_in[0:1])) > 0.0).astype(jnp.int32)
 
@@ -535,6 +531,11 @@
             @pl.when(jnp.logical_not(inner))
             def _():
                 share_z(w, i).wait_send()
+
+    share_home(0, 0).wait_recv()
+    total[...] += matmul_t(list_hot[0], list_back[0])
+    share_home(2, 0).wait_recv()
+    out_ref[...] = (total[...] + matmul_t(list_hot[1], list_back[1])).astype(out_ref.dtype)
 
 
 def solution(mesh):

time: 113 us -> 111 us (0.982)
  the two profiles are of different devices: /device:TPU:1 before, /device:TPU:11 now
where the time goes in v7:
time: 111 us
  Pallas kernels  109 us (98%)
  other arithmetic  1.47 us (1%)
    pallas_call x1, Pallas kernels, local_layer(): pl.pallas_call(functools.partial(packed_kernel, slot_count), out_shape=(p...  109 us

profile of v7, /device:TPU:11, one launch (start us, length us, event | category | flops | bytes accessed | tf_op | source)
XLA Modules:
  0.0 110.7 jit_solution(4610041480964310050)
XLA Ops:
  0.0 0.0 copy-start
  0.0 0.0 copy-start.1
  0.0 0.0 copy-start.2
  0.0 0.0 copy-start.3
  0.0 108.6 %packed_layer.1 = (bf16[1024,768]{1,0:T(8,128)(2,1)S(1)}, s32[1,1]{1,0:T(1,128)}) custom-call(bf16[1024,768]{1,0:T(8,128)(2,1)} %tok_ref.1, s32[1,1024]{1,0:T(1,128)} %bitcast.4, s32[1,1024]{1,0:T(1,128)} %bitcast.6, bf16[1,768,3072]{2,1,0:T(8,128)(2,1)} %gate_hbm.1, bf16[1,768,3072]{2,1,0:T(8,128)(2,1)} %up_hbm.1, bf16[1,3072,768]{2,1,0:T(8,128)(2,1)} %down_hbm.1), custom_call_target="tpu_custom_call" | custom-call | tf_op jit(solution)/shard_map/packed_layer/pallas_call | solution.py:582
  109.1 0.0 copy-done
  109.2 0.0 copy-done.1
  109.2 0.0 copy-done.2
  109.2 0.0 copy-done.3
  109.2 1.5 %fusion = bf16[1024,768]{1,0:T(8,128)(2,1)} fusion(bf16[1024,768]{1,0:T(8,128)(2,1)S(1)} %get-tuple-element.52, f32[1024]{0:T(1024)S(1)} %bitcast.8), kind=kLoop, calls=%fused_computation.1 | loop fusion | flops 2359296 | bytes 3149824 | tf_op jit(solution)/shard_map/cond/branch_0_fun/convert_element_type | solution.py:568
  (1 shorter events, 0.0 us)
Async XLA Ops:
  0.0 109.2 %copy-start = (bf16[1024,768]{1,0:T(8,128)(2,1)S(1)}, bf16[1024,768]{1,0:T(8,128)(2,1)}, u32[]{:S(2)}) copy-start(bf16[1024,768]{1,0:T(8,128)(2,1)} %tok_ref.1) | copy-start | bytes 4718596
  0.0 109.2 %copy-start.1 = (s32[1024,1]{0,1:T(1,128)S(1)}, s32[1024,1]{0,1:T(1,128)}, u32[]{:S(2)}) copy-start(s32[1024,1]{0,1:T(1,128)} %param.10) | copy-start | bytes 12292
  0.0 109.2 %copy-start.2 = (s32[1024,1]{0,1:T(1,128)S(1)}, s32[1024,1]{0,1:T(1,128)}, u32[]{:S(2)}) copy-start(s32[1024,1]{0,1:T(1,128)} %param.12) | copy-start | bytes 12292
  0.0 109.2 %copy-start.3 = (f32[1024,1]{0,1:T(1,128)S(1)}, f32[1024,1]{0,1:T(1,128)}, u32[]{:S(2)}) copy-start(f32[1024,1]{0,1:T(1,128)} %param.11) | copy-start | bytes 12292

commit v8 on v7

--- a/solution.py
+++ b/solution.py
@@ -18,7 +18,7 @@
 INNER = dict(order="oollolloffffnnnn", near=(0, 0, 0, 0), to_inner=(5, 5, 6, 6), to_outer=(6, 6, 7, 7),
              near_back=(14, 15, 16, 16), home=(13, 16), lists=((0, 0, 2), (2, 0, 2), (0, 1, 5), (2, 1, 5)))
 OUTER = dict(order="oooonnnnllllffff", near=(0, 0, 0, 0), to_inner=(4, 4, 4, 4), to_outer=(8, 8, 8, 8),
-             near_back=(10, 10, 13, 13))
+             near_back=(10, 11, 12, 13))
 KINDS = "onfl"
 
 
@@ -178,8 +178,8 @@
     lax.fori_loop(REMOTE + 1, steps, drain, 0)
 
 
-def packed_kernel(slot_count, tok_ref, ids_ref, slots_ref, gate_hbm, up_hbm, down_hbm, out_ref, full_ref,
-                  gate_w, up_w, down_w, hidden, total,
+def packed_kernel(slot_count, tok_hbm, ids_ref, slots_ref, gate_hbm, up_hbm, down_hbm, out_ref, full_ref,
+                  tok_ref, gate_w, up_w, down_w, hidden, total,
                   own_hot, own_send, own_recv, own_result, own_back,
                   z_hot, z_send, z_recv, z_result, z_back,
                   list_hot, list_send, lists, codes_out, codes_in, shares, core_in, z_in, list_back,
@@ -198,6 +198,8 @@
         return carry
 
     lax.fori_loop(1, 16, greet, 0)
+    tok_load = pltpu.make_async_copy(tok_hbm, tok_ref, w_sem.at[3])
+    tok_load.start()
     loads = load_weights((gate_hbm, up_hbm, down_hbm), (gate_w, up_w, down_w), w_sem)
 
     def own_copy(w):
@@ -267,6 +269,7 @@
     before = one_hot(lax.broadcasted_iota(jnp.int32, (folds, folds), 1) < lax.broadcasted_iota(jnp.int32, (folds, folds), 0))
     codes = jnp.concatenate([ids, slots] + [jnp.zeros_like(ids)] * (CODES - 2), axis=0).astype(jnp.float32).astype(jnp.bfloat16)
     excess = 0.0
+    tok_load.wait()
     for h in range(2):
         column = (expert // 2 + h) % 2
         spills = jnp.logical_and(far_spill, ids // 2 % 2 == column).astype(jnp.float32)
@@ -293,12 +296,9 @@
 
         return carry
 
-    lax.fori_loop(0, 4, own_pick, 0)
     pl.semaphore_wait(barrier, 16)
     list_out(0).start()
     list_out(1).start()
-    for w in (2, 3, 1):
-        own_copy(w).start()
 
     def flag_out(q, carry):
         flag_copy(q).start()
@@ -322,6 +322,9 @@
         return carry
 
     lax.fori_loop(0, 4, z_pick, 0)
+    lax.fori_loop(0, 4, own_pick, 0)
+    for w in range(1, 4):
+        own_copy(w).start()
     for w in range(4):
         for i in range(2):
             lists[w, i, SPILL:PADDED] = jnp.zeros((PADDED - SPILL, width), jnp.bfloat16)
@@ -582,15 +585,15 @@
         picked, full = pl.pallas_call(
             functools.partial(packed_kernel, slot_count),
             out_shape=(picked_shape, jax.ShapeDtypeStruct((1, 1), jnp.int32)),
-            in_specs=[vmem] * 3 + [hbm] * 3, out_specs=(vmem, smem),
-            scratch_shapes=weights + [hidden, total]
+            in_specs=[hbm] + [vmem] * 2 + [hbm] * 3, out_specs=(vmem, smem),
+            scratch_shapes=[bf16(rows, width)] + weights + [hidden, total]
             + [bf16(4, slot_count, rows)] + [bf16(*own)] * 4
             + [bf16(4, 2 * BASE + slot_count, rows)] + [bf16(*zed)] * 4
             + [bf16(2, PADDED, rows), bf16(2, PADDED, width), bf16(4, 2, PADDED, width),
                pltpu.VMEM((2, 8, PADDED), jnp.float32), pltpu.VMEM((4, 2, 8, PADDED), jnp.float32), bf16(4, 2, PADDED, width),
                bf16(2, 2, PADDED, width), bf16(2, 2, PADDED, width), bf16(2, PADDED, width)]
             + [flag, pltpu.VMEM((16, 8, 128), jnp.float32), flag, flag]
-            + [dma((3,)), dma((4, 4)), dma((4, 12)), dma((18,)), dma((18,)), dma((18,)), dma((2, 16))],
+            + [dma((4,)), dma((4, 4)), dma((4, 12)), dma((18,)), dma((18,)), dma((18,)), dma((2, 16))],
             compiler_params=params(0), name="packed_layer",
         )(*operands)
         return lax.cond(full[0, 0] > 0, lambda: scaled(padded()), lambda: scaled(picked))

time: 111 us -> 110 us (level)
  no operation moved by 1% of the time
where the time goes in v8:
time: 110 us
  Pallas kernels  108 us (98%)
  other arithmetic  1.47 us (1%)
    pallas_call x1, Pallas kernels, local_layer(): pl.pallas_call(functools.partial(packed_kernel, slot_count), out_shape=(p...  108 us

profile of v8, /device:TPU:11, one launch (start us, length us, event | category | flops | bytes accessed | tf_op | source)
XLA Modules:
  0.0 109.8 jit_solution(7621530459786166600)
XLA Ops:
  0.0 0.0 copy-start
  0.0 0.0 copy-start.1
  0.0 0.0 copy-start.2
  0.0 0.0 copy-start.3
  0.0 107.7 %packed_layer.1 = (bf16[1024,768]{1,0:T(8,128)(2,1)S(1)}, s32[1,1]{1,0:T(1,128)}) custom-call(bf16[1024,768]{1,0:T(8,128)(2,1)} %tok_hbm.1, s32[1,1024]{1,0:T(1,128)} %bitcast.4, s32[1,1024]{1,0:T(1,128)} %bitcast.6, bf16[1,768,3072]{2,1,0:T(8,128)(2,1)} %gate_hbm.1, bf16[1,768,3072]{2,1,0:T(8,128)(2,1)} %up_hbm.1, bf16[1,3072,768]{2,1,0:T(8,128)(2,1)} %down_hbm.1), custom_call_target="tpu_custom_call" | custom-call | tf_op jit(solution)/shard_map/packed_layer/pallas_call | solution.py:585
  108.3 0.0 copy-done
  108.3 0.0 copy-done.1
  108.3 0.0 copy-done.2
  108.3 0.0 copy-done.3
  108.3 1.5 %fusion = bf16[1024,768]{1,0:T(8,128)(2,1)} fusion(bf16[1024,768]{1,0:T(8,128)(2,1)S(1)} %get-tuple-element.52, f32[1024]{0:T(1024)S(1)} %bitcast.8), kind=kLoop, calls=%fused_computation.1 | loop fusion | flops 2359296 | bytes 3149824 | tf_op jit(solution)/shard_map/cond/branch_0_fun/convert_element_type | solution.py:571
  (1 shorter events, 0.0 us)
Async XLA Ops:
  0.0 108.3 %copy-start = (bf16[1024,768]{1,0:T(8,128)(2,1)S(1)}, bf16[1024,768]{1,0:T(8,128)(2,1)}, u32[]{:S(2)}) copy-start(bf16[1024,768]{1,0:T(8,128)(2,1)} %tok_hbm.1) | copy-start | bytes 4718596
  0.0 108.3 %copy-start.1 = (s32[1024,1]{0,1:T(1,128)S(1)}, s32[1024,1]{0,1:T(1,128)}, u32[]{:S(2)}) copy-start(s32[1024,1]{0,1:T(1,128)} %param.10) | copy-start | bytes 12292
  0.0 108.3 %copy-start.2 = (s32[1024,1]{0,1:T(1,128)S(1)}, s32[1024,1]{0,1:T(1,128)}, u32[]{:S(2)}) copy-start(s32[1024,1]{0,1:T(1,128)} %param.12) | copy-start | bytes 12292
  0.0 108.3 %copy-start.3 = (f32[1024,1]{0,1:T(1,128)S(1)}, f32[1024,1]{0,1:T(1,128)}, u32[]{:S(2)}) copy-start(f32[1024,1]{0,1:T(1,128)} %param.11) | copy-start | bytes 12292
